TPU v7x, 256 devices: a whole 4x4x8 slice. The times are simulated.
256 devices in a mesh: row: 16 (over z, core), col: 16 (over y, x).
Axes of the slice: x: 4, y: 4, z: 8, core: 2. Of those that a mesh axis runs over, the one named last changes fastest.
Arguments:
- velocity: float32 [1, 3, 128, 256, 256], P(None, None, 'row', 'col'), may hold values from -6 to 6
- tendency: float32 [1, 3, 128, 256, 256], P(None, None, 'row', 'col'), may hold values from -6 to 6
- step_size: float32 [1], replicated, may hold values from 0.1 to 0.6
- lift_weight: float32 [32, 3], replicated, may hold values from -3.5 to 3.5
- lift_bias: float32 [32], replicated, may hold values from -3 to 3
- spectral_weight: bfloat16 [2, 32, 32, 32, 1024], P(None, 'row', 'col'), may hold values from -6 to 6
- local_weight: float32 [32, 32], replicated, may hold values from -1 to 1
- local_bias: float32 [32], replicated, may hold values from -3 to 3
Outputs:
- features: bfloat16 [1, 32, 128, 256, 256], P(None, None, 'row', 'col')
All inputs are finite; a program needn't handle non-finite values.
Results may differ from a plain program's by a relative error of at most 0.001.
Values sent between devices are 32-bit elements; how exact they have to be, the bound alone decides.
A program may use at most 64 MiB of HBM per device.

v0:
```python
import math

import jax
import jax.numpy as jnp
from jax import lax
from jax.sharding import PartitionSpec as P

KX = 32
KY = 32
KZ = 32
NZ = 256


def wavenumbers(count):
    index = jnp.arange(count, dtype=jnp.int32)
    return jnp.where(index < count // 2, index, index - count)


def angles(waves, points, length):
    return jnp.mod(waves[:, None] * points[None, :], length).astype(jnp.float32) * (
        2.0 * math.pi / length
    )


def forward_table(angle):
    cosine = jnp.cos(angle)
    sine = jnp.sin(angle)
    return jnp.stack([jnp.stack([cosine, -sine], 0), jnp.stack([sine, cosine], 0)], 0)


def inverse_table(angle):
    cosine = jnp.cos(angle)
    sine = jnp.sin(angle)
    return jnp.stack([jnp.stack([cosine, sine], 0), jnp.stack([-sine, cosine], 0)], 0)


def per_device(
    velocity, tendency, step_size, lift_weight, lift_bias, spectral_weight, local_weight, local_bias
):
    highest = lax.Precision.HIGHEST
    samples = velocity.shape[0]
    rows_x = velocity.shape[2]
    rows_y = velocity.shape[3]
    channels = lift_weight.shape[0]
    row_count = lax.axis_size("row")
    col_count = lax.axis_size("col")
    full_x = rows_x * row_count
    full_y = rows_y * col_count
    kz_local = KZ // col_count
    ky_local = KY // row_count
    advanced = velocity + step_size[:, None, None, None, None] * tendency
    width_in = advanced.shape[1]
    z_angle = angles(jnp.arange(KZ, dtype=jnp.int32), jnp.arange(NZ, dtype=jnp.int32), NZ)
    z_table = jnp.stack([jnp.cos(z_angle), -jnp.sin(z_angle)], 0).reshape(
        2, col_count, kz_local, NZ
    )
    z_modes = jnp.einsum("bcxyz,rdkz->bcxdrky", advanced, z_table, precision=highest)
    y_angle = angles(wavenumbers(KY), jnp.arange(full_y, dtype=jnp.int32), full_y)
    outgoing = z_modes.reshape(samples, width_in, rows_x, col_count, -1)
    arrived = lax.all_to_all(outgoing, "col", split_axis=3, concat_axis=3, tiled=True)
    arrived = arrived.reshape(samples, width_in, rows_x, col_count, 2, kz_local, rows_y)
    y_table = forward_table(y_angle).reshape(2, 2, row_count, ky_local, col_count, rows_y)
    by_y = jnp.einsum("bcxsrky,rtdlsy->bcdtklx", arrived, y_table, precision=highest)
    by_y = by_y.reshape(samples, width_in, row_count, -1)
    pencils_x = lax.all_to_all(by_y, "row", split_axis=2, concat_axis=2, tiled=True)
    pencils_x = pencils_x.reshape(samples, width_in, row_count, 2, kz_local, ky_local, rows_x)
    x_angle = angles(wavenumbers(KX), jnp.arange(full_x, dtype=jnp.int32), full_x)
    x_table = forward_table(x_angle).reshape(2, 2, KX, row_count, rows_x)
    coeffs = jnp.einsum("bcsrklx,rtasx->bctkal", pencils_x, x_table, precision=highest)
    coeffs = coeffs * (1.0 / (full_x * full_y * NZ))
    part_index = jnp.arange(2, dtype=jnp.int32)[:, None, None, None]
    kz_global = (
        lax.axis_index("col") * kz_local
        + jnp.arange(kz_local, dtype=jnp.int32)[None, :, None, None]
    )
    kx_index = jnp.arange(KX, dtype=jnp.int32)[None, None, :, None]
    ky_global = (
        lax.axis_index("row") * ky_local
        + jnp.arange(ky_local, dtype=jnp.int32)[None, None, None, :]
    )
    zero_mode = ((part_index == 0) & (kz_global == 0) & (kx_index == 0) & (ky_global == 0)).astype(
        jnp.float32
    )
    coeffs = jnp.einsum("ij,bjtkal->bitkal", lift_weight, coeffs, precision=highest)
    coeffs = coeffs + lift_bias[None, :, None, None, None, None] * zero_mode[None, None]
    weights = spectral_weight.astype(jnp.float32).reshape(
        2, ky_local, kz_local, KX, channels, channels
    )

    def mixing(weight_part, data_part):
        return jnp.einsum("lkaoi,bikal->bokal", weight_part, data_part, precision=highest)

    coef_real = coeffs[:, :, 0]
    coef_imag = coeffs[:, :, 1]
    mixed_real = mixing(weights[0], coef_real) - mixing(weights[1], coef_imag)
    mixed_imag = mixing(weights[0], coef_imag) + mixing(weights[1], coef_real)
    mixed = jnp.stack([mixed_real, mixed_imag], 2)
    x_back = inverse_table(x_angle).reshape(2, 2, KX, row_count, rows_x)
    cells_x = jnp.einsum("botkal,tuadx->boduklx", mixed, x_back, precision=highest)
    cells_x = cells_x.reshape(samples, channels, row_count, -1)
    by_cells = lax.all_to_all(cells_x, "row", split_axis=2, concat_axis=2, tiled=True)
    by_cells = by_cells.reshape(samples, channels, row_count, 2, kz_local, ky_local, rows_x)
    y_back_table = inverse_table(y_angle).reshape(2, 2, row_count, ky_local, col_count, rows_y)
    cells_y = jnp.einsum("bosuklx,uvsldy->bodvkxy", by_cells, y_back_table, precision=highest)
    cells_y = cells_y.reshape(samples, channels, col_count, -1)
    pencils_z = lax.all_to_all(cells_y, "col", split_axis=2, concat_axis=2, tiled=True)
    pencils_z = pencils_z.reshape(samples, channels, col_count, 2, kz_local, rows_x, rows_y)
    doubling = jnp.where(jnp.arange(KZ, dtype=jnp.int32) == 0, 1.0, 2.0).astype(jnp.float32)[
        :, None
    ]
    z_back = jnp.stack([doubling * jnp.cos(z_angle), -doubling * jnp.sin(z_angle)], 0).reshape(
        2, col_count, kz_local, NZ
    )
    spectral = jnp.einsum("bodvkxy,vdkz->boxyz", pencils_z, z_back, precision=highest)
    combined = jnp.dot(local_weight, lift_weight, precision=highest)
    offset = jnp.dot(local_weight, lift_bias, precision=highest) + local_bias
    local_term = (
        jnp.einsum("oj,bjxyz->boxyz", combined, advanced, precision=highest)
        + offset[None, :, None, None, None]
    )
    return jax.nn.gelu(spectral + local_term).astype(jnp.bfloat16)


def solution(mesh):
    in_specs = (
        P(None, None, "row", "col", None),
        P(None, None, "row", "col", None),
        P(),
        P(),
        P(),
        P(None, "row", "col", None, None),
        P(),
        P(),
    )
    out_specs = P(None, None, "row", "col", None)
    return jax.shard_map(
        per_device, mesh=mesh, in_specs=in_specs, out_specs=out_specs, check_vma=False
    )
```

profile of v0, /device:TPU:1, one launch (start us, length us, event | category | flops | bytes accessed | tf_op | source)
XLA Modules:
  0.0 137.8 jit_solution(3150622637888036031)
XLA Ops:
  0.7 0.2 broadcast_multiply_fusion.1
  0.9 3.0 %convolution_bitcast_fusion.1 = f32[1,3,8,16,2,2,16]{6,3,2,1,5,4,0:T(8,128)S(1)} fusion(f32[1,3,8,16,256]{4,3,2,1,0:T(8,128)} %param.8, f32[1,3,8,16,256]{4,3,2,1,0:T(8,128)} %param.9, f32[]{:T(128)} %bitcast.186, f32[1,16,2,256]{3,1,2,0:T(8,128)S(1)} %get-tuple-element.17, f32[1,16,2,256]{3,1,2,0:T(8,128)S(1)} %get-tuple-element.16), kind=kOutput, calls=%fused_computation.16 | convolution fusion | flops 75710464 | bytes 950276 | tf_op jit(solution)/shard_map/bcxyz,rdkz->bcxdrky/dot_general | solution.py:57
  4.0 0.6 copy.77
  4.6 0.6 reshape.643
  5.2 0.8 reshape.645
  6.0 7.6 %all-to-all-start = ((f32[16,1,1536]{2,1,0:T(1,128)}), f32[16,1,1536]{2,1,0:T(1,128)S(1)}, u32[]{:S(2)}, u32[]{:S(2)}) async-start(f32[16,1,1536]{2,1,0:T(1,128)} %reshape.645), calls=%async_computation | async-start | bytes 196608 | tf_op jit(solution)/shard_map/all_to_all | solution.py:60
  13.7 1.1 fusion.49
  14.9 0.3 fusion.69
  15.4 4.9 %all-to-all-done = f32[16,1,1536]{2,1,0:T(1,128)S(1)} async-done(((f32[16,1,1536]{2,1,0:T(1,128)}), f32[16,1,1536]{2,1,0:T(1,128)S(1)}, u32[]{:S(2)}, u32[]{:S(2)}) %all-to-all-start) | async-done | bytes 98336 | tf_op jit(solution)/shard_map/all_to_all | solution.py:60
  20.3 0.6 broadcast.866
  20.9 0.9 reduce
  21.8 0.1 reshape.646
  21.9 0.6 reshape.644
  22.6 4.7 %convolution_bitcast_fusion.4 = f32[1,3,16,2,2,2,8]{2,6,4,1,5,3,0:T(8,128)S(1)} fusion(f32[1,1,16,2,16,16]{5,2,4,0,3,1:T(8,128)S(1)} %get-tuple-element.11, f32[1,1,16,2,16,16]{5,2,4,0,3,1:T(8,128)S(1)} %get-tuple-element.9, f32[1,1,16,2,16,16]{5,2,4,0,3,1:T(8,128)S(1)} %get-tuple-element.10, f32[3,8,16,2,2,16,1,1]{5,4,3,1,0,2,7,6:T(2,128)S(1)} %bitcast.193), kind=kOutput, calls=%fused_computation.20 | convolution fusion | flops 18972672 | bytes 208896 | tf_op jit(solution)/shard_map/bcxsrky,rtdlsy->bcdtklx/dot_general | solution.py:63
  27.3 0.8 reduce.1
  28.1 0.7 reshape.647
  28.8 10.5 %all-to-all-start.1 = ((f32[16,1,192]{2,1,0:T(1,128)}), f32[16,1,192]{2,1,0:T(1,128)S(1)}, u32[]{:S(2)}, u32[]{:S(2)}) async-start(f32[16,1,192]{2,1,0:T(1,128)} %reshape.647), calls=%async_computation.1 | async-start | bytes 32768 | tf_op jit(solution)/shard_map/all_to_all | solution.py:65
  39.4 0.8 squeeze.4
  40.2 0.8 squeeze.5
  40.9 5.7 %all-to-all-done.1 = f32[16,1,192]{2,1,0:T(1,128)S(1)} async-done(((f32[16,1,192]{2,1,0:T(1,128)}), f32[16,1,192]{2,1,0:T(1,128)S(1)}, u32[]{:S(2)}, u32[]{:S(2)}) %all-to-all-start.1) | async-done | bytes 12320 | tf_op jit(solution)/shard_map/all_to_all | solution.py:65
  46.7 0.7 reduce.2
  47.5 0.1 copy.33
  47.6 0.6 fusion.10
  48.2 0.4 fusion.8
  48.6 1.7 %fusion.26 = f32[2,32,2,1,32]{4,3,2,1,0:T(1,128)S(1)} fusion(bf16[2,2,32,32,32]{4,3,2,1,0:T(8,128)(2,1)S(1)} %squeeze.4, f32[32,2,32,2,1]{0,2,3,1,4:T(8,128)S(1)} %get-tuple-element.8), kind=kOutput, calls=%fused_computation.40 | convolution fusion | flops 1572864 | bytes 294912 | tf_op jit(solution)/shard_map/lkaoi,bikal->bokal/dot_general | solution.py:91
  50.3 1.7 %fusion.24 = f32[2,32,2,1,32]{4,3,2,1,0:T(1,128)S(1)} fusion(bf16[2,2,32,32,32]{4,3,2,1,0:T(8,128)(2,1)S(1)} %squeeze.4, f32[32,2,32,2,1]{0,2,3,1,4:T(8,128)S(1)} %get-tuple-element.7), kind=kOutput, calls=%fused_computation.38 | convolution fusion | flops 1572864 | bytes 294912 | tf_op jit(solution)/shard_map/lkaoi,bikal->bokal/dot_general | solution.py:91
  52.1 1.7 %fusion.22 = f32[2,32,2,1,32]{4,3,2,1,0:T(1,128)S(1)} fusion(bf16[2,2,32,32,32]{4,3,2,1,0:T(8,128)(2,1)S(1)} %squeeze.5, f32[32,2,32,2,1]{0,2,3,1,4:T(8,128)S(1)} %get-tuple-element.7), kind=kOutput, calls=%fused_computation.36 | convolution fusion | flops 1572864 | bytes 294912 | tf_op jit(solution)/shard_map/lkaoi,bikal->bokal/dot_general | solution.py:91
  53.8 1.7 %fusion.20 = f32[2,32,2,1,32]{4,3,2,1,0:T(1,128)S(1)} fusion(bf16[2,2,32,32,32]{4,3,2,1,0:T(8,128)(2,1)S(1)} %squeeze.5, f32[32,2,32,2,1]{0,2,3,1,4:T(8,128)S(1)} %get-tuple-element.8), kind=kOutput, calls=%fused_computation.34 | convolution fusion | flops 1572864 | bytes 294912 | tf_op jit(solution)/shard_map/lkaoi,bikal->bokal/dot_general | solution.py:91
  55.7 0.1 copy.62
  55.9 0.6 convolution_bitcast_fusion.2
  56.5 0.3 copy.36
  56.8 0.2 copy.37
  57.0 0.2 reshape.649
  57.2 12.0 %all_to_all.20 = f32[16,1,2048]{2,1,0:T(1,128)S(1)} all-to-all(f32[16,1,2048]{2,1,0:T(1,128)S(1)} %reshape.649), channel_id=1, replica_groups=mesh['row'=16,'col'=16] {'row'}, dimensions={0} | all-to-all | bytes 262144 | tf_op jit(solution)/shard_map/all_to_all | solution.py:101
  69.2 1.0 reduce.3
  70.2 0.1 reshape.650
  70.3 0.2 copy.38
  70.5 3.6 %convolution_bitcast_fusion = f32[1,32,16,2,2,8,16]{1,6,5,4,2,3,0:T(8,128)S(1)} fusion(f32[32,16,2,2,2,8,1,1]{0,5,4,3,2,1,7,6:T(8,128)S(1)} %bitcast.190, f32[1,1,16,2,16,16]{5,2,4,0,3,1:T(8,128)S(1)} %get-tuple-element.11, f32[1,1,16,2,16,16]{5,2,4,0,3,1:T(8,128)S(1)} %get-tuple-element.10, f32[1,1,16,2,16,16]{5,2,4,0,3,1:T(8,128)S(1)} %get-tuple-element.9), kind=kOutput, calls=%fused_computation.11 | convolution fusion | flops 201424896 | bytes 1277952 | tf_op jit(solution)/shard_map/bosuklx,uvsldy->bodvkxy/dot_general | solution.py:104
  74.2 2.2 %copy.41 = f32[1,32,16,2,2,8,16]{1,6,5,4,3,2,0:T(8,128)} copy(f32[1,32,16,2,2,8,16]{1,6,5,4,2,3,0:T(8,128)S(1)} %convolution_bitcast_fusion) | data formatting | bytes 2097152 | tf_op jit(solution)/shard_map/bosuklx,uvsldy->bodvkxy/transpose | solution.py:104
  76.4 3.7 %copy.42 = f32[1,32,16,512]{3,1,0,2:T(8,128)} copy(f32[1,32,16,512]{1,3,2,0:T(8,128)} %bitcast.188) | data formatting | bytes 2097152 | tf_op jit(solution)/shard_map/reshape | solution.py:105
  80.1 3.7 %all-to-all-start.3 = ((f32[1,32,16,512]{3,1,0,2:T(8,128)}), f32[1,32,16,512]{3,1,0,2:T(8,128)S(1)}, u32[]{:S(2)}, u32[]{:S(2)}) async-start(f32[1,32,16,512]{3,1,0,2:T(8,128)} %copy.42), calls=%async_computation.3 | async-start | bytes 2097152 | tf_op jit(solution)/shard_map/all_to_all | solution.py:106
  83.8 0.1 convolution_bitcast_fusion.6
  83.9 0.1 fusion.11
  84.1 5.0 %fusion.30 = f32[8,16,256,32]{2,3,1,0:T(8,128)} fusion(f32[32,3,1,1]{0,1,3,2:T(4,128)S(1)} %convolution_bitcast_fusion.6, f32[3,8,16,256]{3,2,1,0:T(8,128)S(1)} %fusion.44), kind=kOutput, calls=%fused_computation.44 | convolution fusion | flops 37748736 | bytes 4587904 | tf_op jit(solution)/shard_map/oj,bjxyz->boxyz/dot_general | solution.py:118
  89.2 14.5 %all-to-all-done.3 = f32[1,32,16,512]{3,1,0,2:T(8,128)S(1)} async-done(((f32[1,32,16,512]{3,1,0,2:T(8,128)}), f32[1,32,16,512]{3,1,0,2:T(8,128)S(1)}, u32[]{:S(2)}, u32[]{:S(2)}) %all-to-all-start.3) | async-done | bytes 1048608 | tf_op jit(solution)/shard_map/all_to_all | solution.py:106
  103.7 2.6 %copy.43 = f32[1,32,16,512]{1,3,2,0:T(8,128)} copy(f32[1,32,16,512]{3,1,0,2:T(8,128)S(1)} %all-to-all-done.3) | data formatting | bytes 2097152 | tf_op jit(solution)/shard_map/all_to_all | solution.py:106
  106.3 9.1 %copy.44 = f32[32,16,2,2,8,16]{1,5,2,3,4,0:T(8,128)} copy(f32[32,16,2,2,8,16]{0,5,4,3,2,1:T(8,128)} %bitcast.187) | data formatting | bytes 2097152 | tf_op jit(solution)/shard_map/reshape.46
  115.5 22.3 %fusion.7 = bf16[1,32,8,16,256]{4,3,2,1,0:T(8,128)(2,1)} fusion(f32[8,16,256,32]{2,3,1,0:T(8,128)} %fusion.30, f32[32,16,2,2,8,16]{1,5,2,3,4,0:T(8,128)} %copy.44, f32[32]{0:T(128)S(1)} %fusion.11, f32[1,16,2,256]{3,1,2,0:T(8,128)S(1)} %get-tuple-element.18, f32[1,16,2,256]{3,1,2,0:T(8,128)S(1)} %get-tuple-element.15), kind=kOutput, calls=%fused_computation.8 | convolution fusion | flops 816857088 | bytes 7405696 | tf_op jit(solution)/shard_map/bodvkxy,vdkz->boxyz/dot_general | solution.py:114
  (37 shorter events, 0.9 us)
Async XLA Ops:
  0.0 83.8 %copy-start = (f32[32,32]{1,0:T(8,128)S(1)}, f32[32,32]{1,0:T(8,128)}, u32[]{:S(2)}) copy-start(f32[32,32]{1,0:T(8,128)} %param.14) | copy-start | bytes 12292
  0.0 13.7 %copy-start.3 = (bf16[2,2,2,32,1024]{4,3,2,1,0:T(8,128)(2,1)S(1)}, bf16[2,2,2,32,1024]{4,3,2,1,0:T(8,128)(2,1)}, u32[]{:S(2)}) copy-start(bf16[2,2,2,32,1024]{4,3,2,1,0:T(8,128)(2,1)} %param.13) | copy-start | bytes 1572868
  6.0 14.3 %all-to-all-start = ((f32[16,1,1536]{2,1,0:T(1,128)}), f32[16,1,1536]{2,1,0:T(1,128)S(1)}, u32[]{:S(2)}, u32[]{:S(2)}) async-start(f32[16,1,1536]{2,1,0:T(1,128)} %reshape.645), calls=%async_computation | async-start | bytes 196608 | tf_op jit(solution)/shard_map/all_to_all | solution.py:60
  14.8 33.3 %copy-start.4 = (f32[32,3]{0,1:T(4,128)S(1)}, f32[32,3]{0,1:T(4,128)}, u32[]{:S(2)}) copy-start(f32[32,3]{0,1:T(4,128)} %param.11) | copy-start | bytes 1156
  14.9 33.3 %copy-start.5 = (f32[32]{0:T(128)S(1)}, f32[32]{0:T(128)}, u32[]{:S(2)}) copy-start(f32[32]{0:T(128)} %param.12) | copy-start | bytes 388
  28.8 17.9 %all-to-all-start.1 = ((f32[16,1,192]{2,1,0:T(1,128)}), f32[16,1,192]{2,1,0:T(1,128)S(1)}, u32[]{:S(2)}, u32[]{:S(2)}) async-start(f32[16,1,192]{2,1,0:T(1,128)} %reshape.647), calls=%async_computation.1 | async-start | bytes 32768 | tf_op jit(solution)/shard_map/all_to_all | solution.py:65
  76.4 7.5 %copy-start.6 = (f32[32]{0:T(128)S(1)}, f32[32]{0:T(128)}, u32[]{:S(2)}) copy-start(f32[32]{0:T(128)} %param.15) | copy-start | bytes 388
  76.4 7.6 %copy-start.1 = (f32[1,3,8,16,256]{4,3,2,1,0:T(8,128)S(1)}, f32[1,3,8,16,256]{4,3,2,1,0:T(8,128)}, u32[]{:S(2)}) copy-start(f32[1,3,8,16,256]{4,3,2,1,0:T(8,128)} %param.8) | copy-start | bytes 1179652
  76.4 7.6 %copy-start.2 = (f32[1,3,8,16,256]{4,3,2,1,0:T(8,128)S(1)}, f32[1,3,8,16,256]{4,3,2,1,0:T(8,128)}, u32[]{:S(2)}) copy-start(f32[1,3,8,16,256]{4,3,2,1,0:T(8,128)} %param.9) | copy-start | bytes 1179652
  80.1 23.6 %all-to-all-start.3 = ((f32[1,32,16,512]{3,1,0,2:T(8,128)}), f32[1,32,16,512]{3,1,0,2:T(8,128)S(1)}, u32[]{:S(2)}, u32[]{:S(2)}) async-start(f32[1,32,16,512]{3,1,0,2:T(8,128)} %copy.42), calls=%async_computation.3 | async-start | bytes 2097152 | tf_op jit(solution)/shard_map/all_to_all | solution.py:106
where the time goes:
time: 138 us
  matrix products  47.5 us (34%)
  waiting for transfers between devices  25.2 us (18%)
  local copies, waits for them, and re-layouts  24.9 us (18%)
  starting transfers between devices  21.7 us (16%)
  blocking collectives  12 us (9%)
  other arithmetic  5.42 us (4%)
    dot_general x1, matrix products, per_device(): jnp.einsum('bodvkxy,vdkz->boxyz', pencils_z, z_back, precision=highest)  22.3 us
    all_to_all x1, waiting for transfers between devices, per_device(): lax.all_to_all(cells_y, 'col', split_axis=2, concat_axis=2, tiled=True)  14.5 us
    all_to_all x1, blocking collectives, per_device(): lax.all_to_all(cells_x, 'row', split_axis=2, concat_axis=2, tiled=True)  12 us
    all_to_all x1, starting transfers between devices, per_device(): lax.all_to_all(by_y, 'row', split_axis=2, concat_axis=2, tiled=True)  10.5 us
    another operation x3, local copies, waits for them, and re-layouts  9.77 us
    all_to_all x1, starting transfers between devices, per_device(): lax.all_to_all(outgoing, 'col', split_axis=3, concat_axis=3, tiled=True)  7.57 us
    dot_general x4, matrix products, mixing(): jnp.einsum('lkaoi,bikal->bokal', weight_part, data_part, precision=highest)  6.93 us
    all_to_all x1, waiting for transfers between devices, per_device(): lax.all_to_all(by_y, 'row', split_axis=2, concat_axis=2, tiled=True)  5.71 us
  transfers between devices with their start and end apart: 3, of which 3 were waited for; matrix products, arithmetic and copies ran while one was open for 6% of the time, Pallas kernels for 0%

commit v1 on v0

v1 whole, which is shorter than its diff:
```python
import functools
import math

import jax
import jax.numpy as jnp
import numpy as np
from jax import lax
from jax.experimental import pallas as pl
from jax.experimental.pallas import tpu as pltpu
from jax.sharding import PartitionSpec as P

F32 = jnp.float32
BF16 = jnp.bfloat16
MESH = pl.DeviceIdType.MESH
N = 16


def split(x):
    hi = x.astype(BF16)
    lo = (x - hi.astype(F32)).astype(BF16)
    return hi, lo


def dot(a, b):
    return jnp.dot(a, b, preferred_element_type=F32)


def dot_nt(a, b):
    return lax.dot_general(a, b, (((1,), (1,)), ((), ())), preferred_element_type=F32)


def np_split(x):
    x = np.asarray(x, np.float64)
    hi = x.astype(np.float32).astype(jnp.bfloat16)
    lo = (x - hi.astype(np.float64)).astype(np.float32).astype(jnp.bfloat16)
    return hi, lo


@functools.lru_cache(None)
def tables():
    turn = 2.0 * np.pi
    ix = np.arange
    waves = np.where(ix(32) < 16, ix(32), ix(32) - 32)
    eye8 = np.eye(8)
    z_angle = turn * (ix(32)[:, None] * ix(256)[None, :] % 256) / 256
    z_hi, z_lo = np_split(np.concatenate([np.cos(z_angle), -np.sin(z_angle)], 0))
    fwd_z = np.concatenate([z_hi, z_lo, z_hi], 1)
    a = turn * waves[None, :] * ix(16)[:, None] / 256
    by = np.zeros((2, 8, 16, 2, 32, 8))
    for x in range(8):
        by[0, x, :, 0, :, x] = np.cos(a)
        by[1, x, :, 0, :, x] = np.sin(a)
        by[0, x, :, 1, :, x] = -np.sin(a)
        by[1, x, :, 1, :, x] = np.cos(a)
    by_hi, by_lo = np_split(by.reshape(256, 512))
    b = turn * (waves[None, :] * ix(16)[:, None] % 16) / 16
    b = np.repeat(b, 8, axis=1)
    tw_y = np.stack([np.cos(b), np.sin(b)], 0).astype(np.float32)
    c = turn * waves[None, :] * ix(8)[:, None] / 128
    bx = []
    for quarter in (0.0, np.pi / 2):
        t = np.zeros((2, 8, 8, 8, 2, 32))
        for e in range(8):
            t[0, e, :, e, 0, :] = np.cos(c + quarter)
            t[1, e, :, e, 0, :] = np.sin(c + quarter)
            t[0, e, :, e, 1, :] = -np.sin(c + quarter)
            t[1, e, :, e, 1, :] = np.cos(c + quarter)
        bx.append(t.reshape(128, 512))
    bx = np.stack(bx, 0).astype(np.float32)
    d = turn * (waves[None, :] * ix(16)[:, None] % 16) / 16
    d = np.tile(d, (1, 16))
    tw_x = np.stack([np.cos(d), np.sin(d)], 0).astype(np.float32)
    sel = (ix(1024)[:, None] // 32 == ix(128)[None, :] // 4).astype(jnp.bfloat16)
    f = turn * (waves[None, :] * ix(128)[:, None] % 128) / 128
    ex_hi, ex_lo = np_split(np.concatenate([np.cos(f), np.sin(f)], 1))
    inv_x = np.concatenate([ex_hi, ex_hi, ex_lo], 1)
    g = turn * waves[:, None] * ix(32)[None, :] / 256
    ey = np.zeros((2, 32, 8, 2, 8, 16))
    for x in range(8):
        for blk in range(2):
            ey[0, :, x, blk, x, :] = np.cos(g[:, blk * 16:blk * 16 + 16])
            ey[1, :, x, blk, x, :] = -np.sin(g[:, blk * 16:blk * 16 + 16])
    ey_hi, ey_lo = np_split(ey.reshape(512, 256))
    h = turn * (waves[None, :] * ix(8)[:, None] % 8) / 8
    h = np.repeat(h, 8, axis=1)
    tw_i = np.stack([np.cos(h), np.sin(h)], 0).astype(np.float32)
    ez = np.zeros((16, 2, 2, 2, 2, 256))
    weight = np.where(ix(32) == 0, 1.0, 2.0)[:, None]
    cz = (weight * np.cos(z_angle)).reshape(16, 2, 256)
    sz = (-weight * np.sin(z_angle)).reshape(16, 2, 256)
    for o in range(2):
        ez[:, o, :, 0, o, :] = cz
        ez[:, o, :, 1, o, :] = sz
    ez_hi, ez_lo = np_split(ez.reshape(128, 512))
    inv_z = np.concatenate([ez_hi, ez_hi, ez_lo], 0)
    return dict(
        fwd_z=fwd_z, by=np.stack([by_hi, by_lo], 0), tw_y=tw_y, bx=bx, tw_x=tw_x, sel=sel,
        inv_x=inv_x, ey=np.stack([ey_hi, ey_lo], 0), tw_i=tw_i, inv_z=inv_z,
    )


def forward_z(advanced, fwd_z):
    hi, lo = split(advanced)
    return dot_nt(fwd_z, jnp.concatenate([hi, hi, lo], 1))


def forward_y(arrived, by_hi, by_lo, tw_c, tw_s):
    hi, lo = split(arrived)
    u = dot(jnp.concatenate([hi, lo], 0), by_hi)
    u = u[:128] + u[128:] + dot(hi, by_lo)
    real, imag = jnp.zeros((8, 256), F32), jnp.zeros((8, 256), F32)
    for c in range(N):
        ur, ui = u[8 * c:8 * c + 8, :256], u[8 * c:8 * c + 8, 256:]
        tc, ts = tw_c[c:c + 1, :], tw_s[c:c + 1, :]
        real += ur * tc + ui * ts
        imag += ui * tc - ur * ts
    return real, imag


def x_table(bx0, bx1, tc, ts):
    return split(bx0 * tc + bx1 * ts)


def forward_x(real, imag, bx_hi, bx_lo, roll):
    low = lax.broadcasted_iota(jnp.int32, (8, 128), 1) < 64
    rows = []
    for v in range(2):
        re, im = real[:, 128 * v:128 * v + 128], imag[:, 128 * v:128 * v + 128]
        rows.append(jnp.where(low, re, roll(im, 64, 1)))
        rows.append(jnp.where(low, roll(re, 64, 1), im))
    hi, lo = split(jnp.concatenate(rows, 0))
    u = dot(jnp.concatenate([hi, lo], 0), bx_hi)
    return u[:32] + u[32:] + dot(hi, bx_lo)


def lifted_coeffs(total, first, lift):
    row = lax.broadcasted_iota(jnp.int32, (8, 128), 0)
    lane = lax.broadcasted_iota(jnp.int32, (8, 128), 1)
    total = total * (1.0 / 8388608.0) + jnp.where((row == 3) & (lane == 0), first, 0.0)
    return lax.dot_general(
        total.T, lift, (((1,), (1,)), ((), ())), precision=lax.Precision.HIGHEST,
        preferred_element_type=F32,
    )


def mix(coeffs, weight, sel):
    his, los = [], []
    for ky in range(2):
        for kz in range(2):
            cr = coeffs[64 * ky:64 * ky + 32, 128 * kz:128 * kz + 128]
            ci = coeffs[64 * ky + 32:64 * ky + 64, 128 * kz:128 * kz + 128]
            cr8 = jnp.concatenate([cr] * 8, 1)
            ci8 = jnp.concatenate([ci] * 8, 1)
            wr = weight(0, ky, kz).astype(F32)
            wi = weight(1, ky, kz).astype(F32)
            for value in (wr * cr8 - wi * ci8, wr * ci8 + wi * cr8):
                hi, lo = split(value)
                his.append(hi)
                los.append(lo)
    return dot(jnp.concatenate(his, 0), sel) + dot(jnp.concatenate(los, 0), sel)


def inverse_x(mixed, ky, inv_x):
    kind = lax.broadcasted_iota(jnp.int32, (32, 128), 1) % 4
    block = [mixed[128 * ky + 32 * n:128 * ky + 32 * n + 32] for n in range(4)]

    def pick(a, b, c, d):
        return jnp.where(kind == 0, a, jnp.where(kind == 1, b, jnp.where(kind == 2, c, d)))

    top = pick(block[0], block[1], block[2], block[3])
    bottom = pick(-block[1], block[0], -block[3], block[2])
    hi, lo = split(jnp.concatenate([top, bottom], 0))
    return dot(inv_x, jnp.concatenate([hi, lo, hi], 0))


def turned(arrived, roll):
    even = lax.broadcasted_iota(jnp.int32, arrived.shape, 1) % 2 == 0
    other = jnp.where(even, roll(arrived, 127, 1), -roll(arrived, 1, 1))
    return arrived.T, other.T


def inverse_y(plain, other, tc, ts, ey_hi, ey_lo):
    hi, lo = split(jnp.concatenate([plain * tc - other * ts, other * tc + plain * ts], 1))
    return dot(hi, ey_hi) + dot(lo, ey_hi) + dot(hi, ey_lo)


def inverse_z(block, inv_z):
    hi, lo = split(block.T)
    return dot(jnp.concatenate([hi, lo, hi], 1), inv_z)


def activate(value):
    cubic = value * (0.7978845608028654 + 0.035677408136300125 * (value * value))
    half = 0.5 * value
    return half + half * jnp.tanh(cubic)


def exchange_kernel(
    step_ref, v_hbm, t_hbm, w_hbm, lift_ref, fz_hbm, by_hbm, twy_hbm, bx_hbm, twx_hbm, sel_hbm,
    ix_hbm, ey_hbm, twi_hbm,
    out_ref,
    v_ref, t_ref, w_ref, fz_ref, by_ref, twy_ref, bx_ref, twx_ref, sel_ref, ix_ref, ey_ref, twi_ref,
    s1, r1, s2, r2, s3, r3, s4,
    load_sem, send1, recv1, send2, recv2, send3, recv3, send4, recv4,
):
    r = lax.axis_index("row")
    c = lax.axis_index("col")

    barrier = pltpu.get_barrier_semaphore()
    pairs = [
        (v_hbm, v_ref), (t_hbm, t_ref), (fz_hbm, fz_ref), (by_hbm, by_ref), (twy_hbm, twy_ref),
        (bx_hbm, bx_ref), (twx_hbm, twx_ref), (w_hbm, w_ref), (sel_hbm, sel_ref), (ix_hbm, ix_ref),
        (ey_hbm, ey_ref), (twi_hbm, twi_ref),
    ]
    loads = [
        pltpu.make_async_copy(src, dst, load_sem.at[n]) for n, (src, dst) in enumerate(pairs)
    ]
    for load in loads:
        load.start()
    for d in range(1, N):
        pl.semaphore_signal(
            barrier, inc=1, device_id={"row": r, "col": (c + d) % N}, device_id_type=MESH)
        pl.semaphore_signal(
            barrier, inc=1, device_id={"row": (r + d) % N, "col": c}, device_id_type=MESH)

    for load in loads[:3]:
        load.wait()
    advanced = (v_ref[...] + step_ref[0] * t_ref[...]).reshape(384, 256)
    z = forward_z(advanced, fz_ref[...])
    s1[pl.ds(3, 64, stride=4), :] = jnp.zeros((64, 128), F32)
    for j in range(3):
        s1[pl.ds(j, 64, stride=4), :] = z[:, 128 * j:128 * j + 128]
    pl.semaphore_wait(barrier, 2 * (N - 1))

    def to_col(src, dst, send, recv, d):
        return pltpu.make_async_remote_copy(
            src_ref=src, dst_ref=dst, send_sem=send, recv_sem=recv,
            device_id={"row": r, "col": d}, device_id_type=MESH)

    def to_row(src, dst, send, recv, d):
        return pltpu.make_async_remote_copy(
            src_ref=src, dst_ref=dst, send_sem=send, recv_sem=recv,
            device_id={"row": d, "col": c}, device_id_type=MESH)

    first = []
    for d in range(1, N):
        dest = (c + d) % N
        for part in range(2):
            first.append(to_col(
                s1.at[pl.ds(pl.multiple_of(128 * part + 8 * dest, 8), 8)], r1.at[part, c],
                send1.at[part, d], recv1.at[part, d], dest))
            first[-1].start()
    for part in range(2):
        r1[part, c] = s1[pl.ds(pl.multiple_of(128 * part + 8 * c, 8), 8), :]
    for load in loads[3:]:
        load.wait()
    bx_hi, bx_lo = x_table(
        bx_ref[0], bx_ref[1], twx_ref[0, pl.ds(r, 1), :], twx_ref[1, pl.ds(r, 1), :])
    for copy in first:
        copy.wait_recv()

    arrived = jnp.concatenate([r1[0].reshape(128, 128), r1[1].reshape(128, 128)], 1)
    real, imag = forward_y(arrived, by_ref[0], by_ref[1], twy_ref[0], twy_ref[1])
    partial = forward_x(real, imag, bx_hi, bx_lo, pltpu.roll)
    for g in range(4):
        for k in range(4):
            s2[4 * g + k] = partial[8 * g:8 * g + 8, 128 * k:128 * k + 128]
    second = []
    for d in range(1, N):
        dest = (r + d) % N
        second.append(to_row(s2.at[dest], r2.at[r], send2.at[d], recv2.at[d], dest))
        second[-1].start()
    r2[r] = s2[r]
    for copy in second:
        copy.wait_recv()
    total = jnp.sum(r2[...], axis=0)

    origin = jnp.where((r == 0) & (c == 0), 1.0, 0.0).astype(F32)
    coeffs = lifted_coeffs(total, origin, lift_ref[...])
    mixed = mix(coeffs, lambda part, ky, kz: w_ref[part, ky, kz], sel_ref[...])
    for ky in range(2):
        s3[:, 8 * ky:8 * ky + 8, :] = inverse_x(mixed, ky, ix_ref[...]).reshape(16, 8, 128)
    third = []
    for d in range(1, N):
        dest = (r + d) % N
        third.append(to_row(s3.at[dest], r3.at[r], send3.at[d], recv3.at[d], dest))
        third[-1].start()
    r3[r] = s3[r]
    for copy in third:
        copy.wait_recv()

    plain, other = turned(r3[...].reshape(256, 128), pltpu.roll)
    for k in range(8):
        m = (c // 2 + k) % 8
        h = inverse_y(plain, other, twi_ref[0, pl.ds(m, 1), :], twi_ref[1, pl.ds(m, 1), :],
                      ey_ref[0], ey_ref[1])
        for b in range(2):
            dest = 2 * m + b
            s4[dest] = h[:, 128 * b:128 * b + 128]
            copy = to_col(s4.at[dest], out_ref.at[c], send4.at[dest], recv4.at[c], dest)
            if k > 0:
                copy.start()
            else:
                @pl.when(dest != c)
                def _():
                    copy.start()

    out_ref[c] = s4[c]
    for d in range(1, N):
        source = (c + d) % N
        copy = to_col(s4.at[source], out_ref.at[source], send4.at[source], recv4.at[source], source)
        copy.wait_recv()
        copy.wait_send()
    for copy in first + second + third:
        copy.wait_send()


def cells_kernel(step_ref, local_ref, g_ref, v_ref, t_ref, iz_ref, out_ref, adv_ref):
    @pl.when(pl.program_id(0) == 0)
    def _():
        adv_ref[...] = v_ref[...] + step_ref[0] * t_ref[...]

    base = pl.program_id(0) * 8
    for q in range(4):
        values = inverse_z(g_ref[:, 8 * q:8 * q + 8, :].reshape(128, 128), iz_ref[...])
        for o in range(2):
            index = base + 2 * q + o
            scale = [local_ref[index, j] for j in range(4)]
            for x in range(8):
                cell = slice(16 * x, 16 * x + 16)
                value = values[cell, 256 * o:256 * o + 256] + scale[3]
                for j in range(3):
                    value += scale[j] * adv_ref[j, cell, :]
                out_ref[2 * q + o, x] = activate(value).astype(BF16)


def per_device(
    velocity, tendency, step_size, lift_weight, lift_bias, spectral_weight, local_weight, local_bias
):
    highest = lax.Precision.HIGHEST
    t = tables()
    v = velocity.reshape(3, 128, 256)
    dv = tendency.reshape(3, 128, 256)
    four = jnp.concatenate([lift_weight, lift_bias[:, None]], 1)
    four = jnp.concatenate([four] * 4, 0)
    zero = jnp.zeros((128, 4), F32)
    lift = jnp.concatenate(
        [jnp.concatenate([four, zero], 1), jnp.concatenate([zero, four], 1)], 0)
    local = jnp.dot(local_weight, four[:32], precision=highest)
    local = local + jnp.concatenate([jnp.zeros((32, 3), F32), local_bias[:, None]], 1)

    vmem = pl.BlockSpec(memory_space=pltpu.VMEM)
    smem = pl.BlockSpec(memory_space=pltpu.SMEM)
    anywhere = pl.BlockSpec(memory_space=pl.ANY)
    far = [v, dv, spectral_weight]
    consts = [t[n] for n in ("fwd_z", "by", "tw_y", "bx", "tw_x", "sel", "inv_x", "ey", "tw_i")]
    scratch = [pltpu.VMEM(a.shape, a.dtype) for a in far + consts]
    blocks = pl.pallas_call(
        exchange_kernel,
        out_shape=jax.ShapeDtypeStruct((16, 128, 128), F32),
        in_specs=[smem] + [anywhere] * 3 + [vmem] + [anywhere] * len(consts),
        out_specs=vmem,
        scratch_shapes=scratch + [
            pltpu.VMEM((256, 128), F32), pltpu.VMEM((2, 16, 8, 128), F32),
            pltpu.VMEM((16, 8, 128), F32), pltpu.VMEM((16, 8, 128), F32),
            pltpu.VMEM((16, 16, 128), F32), pltpu.VMEM((16, 16, 128), F32),
            pltpu.VMEM((16, 128, 128), F32),
            pltpu.SemaphoreType.DMA((12,)),
            pltpu.SemaphoreType.DMA((2, 16)), pltpu.SemaphoreType.DMA((2, 16)),
        ] + [pltpu.SemaphoreType.DMA((16,))] * 6,
        compiler_params=pltpu.CompilerParams(
            collective_id=0, has_side_effects=True, vmem_limit_bytes=40 * 1024 * 1024),
        name="exchange",
    )(step_size, *far, lift, *[jnp.asarray(a) for a in consts])

    out = pl.pallas_call(
        cells_kernel,
        grid=(4,),
        out_shape=jax.ShapeDtypeStruct((32, 8, 16, 256), BF16),
        in_specs=[
            smem, smem,
            pl.BlockSpec((16, 32, 128), lambda i: (0, i, 0)),
            pl.BlockSpec((3, 128, 256), lambda i: (0, 0, 0)),
            pl.BlockSpec((3, 128, 256), lambda i: (0, 0, 0)),
            pl.BlockSpec((384, 512), lambda i: (0, 0)),
        ],
        out_specs=pl.BlockSpec((8, 8, 16, 256), lambda i: (i, 0, 0, 0)),
        scratch_shapes=[pltpu.VMEM((3, 128, 256), F32)],
        compiler_params=pltpu.CompilerParams(vmem_limit_bytes=40 * 1024 * 1024),
        name="cells",
    )(step_size, local, blocks, v, dv, jnp.asarray(t["inv_z"]))
    return out.reshape(1, 32, 8, 16, 256)


def solution(mesh):
    in_specs = (
        P(None, None, "row", "col", None),
        P(None, None, "row", "col", None),
        P(),
        P(),
        P(),
        P(None, "row", "col", None, None),
        P(),
        P(),
    )
    out_specs = P(None, None, "row", "col", None)
    return jax.shard_map(
        per_device, mesh=mesh, in_specs=in_specs, out_specs=out_specs, check_vma=False
    )
```

time: 138 us -> 66.6 us (0.48)
  Pallas kernels: 0 us -> 51.4 us
  matrix products: 47.5 us -> 0.84 us
  waiting for transfers between devices: 25.2 us -> 0 us
  starting transfers between devices: 21.7 us -> 0 us
  local copies, waits for them, and re-layouts: 24.9 us -> 12 us
  blocking collectives: 12 us -> 0 us
  other arithmetic: 5.42 us -> 0.92 us
    pallas_call x0 -> x2, Pallas kernels: none -> 51.4 us  [the longest x1 46.3 us: per_device(): pl.pallas_call(exchange_kernel, out_shape=jax.ShapeDtypeStruct((16, 128,...]
    dot_general x14 -> x1, matrix products: 47.5 us -> 0.84 us  [per_device(): local = jnp.dot(local_weight, four[:32], precision=highest)]
    all_to_all x3 -> x0, waiting for transfers between devices: 25.2 us -> none  [the longest x1 14.5 us: per_device(): lax.all_to_all(cells_y, 'col', split_axis=2, concat_axis=2, tiled=True)]
    all_to_all x3 -> x0, starting transfers between devices: 21.7 us -> none  [the longest x1 10.5 us: per_device(): lax.all_to_all(by_y, 'row', split_axis=2, concat_axis=2, tiled=True)]
    all_to_all x1 -> x0, blocking collectives: 12 us -> none  [per_device(): lax.all_to_all(cells_x, 'row', split_axis=2, concat_axis=2, tiled=True)]
    another operation x3 -> x0, local copies, waits for them, and re-layouts: 9.77 us -> none
    unnamed x20 -> x28, local copies, waits for them, and re-layouts: 2 us -> 11.2 us
    reshape x5 -> x0, local copies, waits for them, and re-layouts: 5.16 us -> none  [the longest x1 3.67 us: per_device(): cells_y = cells_y.reshape(samples, channels, col_count, -1)]
  transfers between devices with their start and end apart: 3 -> 0, of which waited for: 3 -> 0; matrix products, arithmetic and copies ran while one was open for 6% -> 0% of each run, Pallas kernels for 0% -> 0%
where the time goes in v1:
time: 66.6 us; the launch traced here: 65.9 us
  Pallas kernels  51.4 us (77%)
  local copies, waits for them, and re-layouts  12 us (18%)
  other arithmetic  0.92 us (1%)
  matrix products  0.84 us (1%)
  between operations  0.72 us (1%)
    pallas_call x1, Pallas kernels, per_device(): pl.pallas_call(exchange_kernel, out_shape=jax.ShapeDtypeStruct((16, 128,...  46.3 us
    unnamed x28, local copies, waits for them, and re-layouts  11.2 us
    pallas_call x1, Pallas kernels, per_device(): pl.pallas_call(cells_kernel, grid=(4,), out_shape=jax.ShapeDtypeStruct((3...  5.11 us

profile of v1, /device:TPU:1, one launch (start us, length us, event | category | flops | bytes accessed | tf_op | source)
XLA Modules:
  0.0 65.9 jit_solution(12336309153143163262)
XLA Ops:
  0.0 0.0 copy-start
  0.7 0.9 %maximum_maximum_fusion = f32[128,4]{0,1:T(4,128)S(1)} fusion(f32[32,1]{0,1:T(1,128)} %bitcast.14, f32[32,3]{0,1:T(4,128)} %param.21), kind=kLoop, calls=%fused_computation.8 | loop fusion | flops 3584 | bytes 2560 | tf_op jit(solution)/shard_map/concatenate | solution.py:345
  1.6 0.7 %copy.24 = f32[32,1]{1,0:T(8,128)S(1)} copy(f32[32,1]{0,1:T(1,128)} %bitcast.16) | data formatting | bytes 256 | tf_op jit(solution)/shard_map/broadcast_in_dim | solution.py:350
  2.3 0.0 copy-done
  2.3 0.8 %fusion.local_ref = f32[32,4]{1,0:T(8,128)S(1)} fusion(f32[32,32]{1,0:T(8,128)S(1)} %copy-done, f32[32,1]{1,0:T(8,128)S(1)} %copy.24, f32[32,1]{0,1:T(1,128)} %bitcast.15, f32[32,3]{0,1:T(4,128)} %param.21), kind=kOutput, calls=%fused_computation.1 | convolution fusion | flops 49408 | bytes 5248 | tf_op jit(solution)/shard_map/dot_general | solution.py:349
  3.2 0.1 copy.25.lift_ref
  3.3 0.0 copy-start.1
  3.3 1.0 %copy-done.1 = f32[1,3,8,16,256]{4,3,2,1,0:T(8,128)S(1)} copy-done((f32[1,3,8,16,256]{4,3,2,1,0:T(8,128)S(1)}, f32[1,3,8,16,256]{4,3,2,1,0:T(8,128)}, u32[]{:S(2)}) %copy-start.1) | copy-done | bytes 393240
  4.3 0.0 copy-start.2
  4.3 1.0 %copy-done.2 = f32[1,3,8,16,256]{4,3,2,1,0:T(8,128)S(1)} copy-done((f32[1,3,8,16,256]{4,3,2,1,0:T(8,128)S(1)}, f32[1,3,8,16,256]{4,3,2,1,0:T(8,128)}, u32[]{:S(2)}) %copy-start.2) | copy-done | bytes 393240
  5.3 0.0 copy-start.3
  5.3 1.0 %copy-done.3 = bf16[2,2,2,32,1024]{4,3,2,1,0:T(8,128)(2,1)S(1)} copy-done((bf16[2,2,2,32,1024]{4,3,2,1,0:T(8,128)(2,1)S(1)}, bf16[2,2,2,32,1024]{4,3,2,1,0:T(8,128)(2,1)}, u32[]{:S(2)}) %copy-start.3) | copy-done | bytes 524312
  6.3 0.0 copy-start.4
  6.3 1.0 %copy-done.4 = bf16[2,512,256]{2,1,0:T(8,128)(2,1)S(1)} copy-done((bf16[2,512,256]{2,1,0:T(8,128)(2,1)S(1)}, bf16[2,512,256]{2,1,0:T(8,128)(2,1)}, u32[]{:S(2)}) %copy-start.4) | copy-done | bytes 524312
  7.4 0.0 copy-start.5
  7.4 1.0 %copy-done.5 = f32[2,128,512]{2,1,0:T(8,128)S(1)} copy-done((f32[2,128,512]{2,1,0:T(8,128)S(1)}, f32[2,128,512]{2,1,0:T(8,128)}, u32[]{:S(2)}) %copy-start.5) | copy-done | bytes 524312
  8.4 0.0 copy-start.6
  8.4 1.0 %copy-done.6 = bf16[2,256,512]{2,1,0:T(8,128)(2,1)S(1)} copy-done((bf16[2,256,512]{2,1,0:T(8,128)(2,1)S(1)}, bf16[2,256,512]{2,1,0:T(8,128)(2,1)}, u32[]{:S(2)}) %copy-start.6) | copy-done | bytes 524312
  9.5 0.0 copy-start.8
  9.5 0.9 %copy-done.8 = bf16[1024,128]{1,0:T(8,128)(2,1)S(1)} copy-done((bf16[1024,128]{1,0:T(8,128)(2,1)S(1)}, bf16[1024,128]{1,0:T(8,128)(2,1)}, u32[]{:S(2)}) %copy-start.8) | copy-done | bytes 262168
  10.4 0.0 copy-start.9
  10.4 0.9 %copy-done.9 = bf16[64,768]{1,0:T(8,128)(2,1)S(1)} copy-done((bf16[64,768]{1,0:T(8,128)(2,1)S(1)}, bf16[64,768]{1,0:T(8,128)(2,1)}, u32[]{:S(2)}) %copy-start.9) | copy-done | bytes 98328
  11.3 0.0 copy-start.10
  11.3 0.8 %copy-done.10 = bf16[128,192]{1,0:T(8,128)(2,1)S(1)} copy-done((bf16[128,192]{1,0:T(8,128)(2,1)S(1)}, bf16[128,192]{1,0:T(8,128)(2,1)}, u32[]{:S(2)}) %copy-start.10) | copy-done | bytes 49176
  12.2 0.0 copy-start.11
  12.2 0.8 %copy-done.11 = f32[2,16,512]{2,1,0:T(8,128)S(1)} copy-done((f32[2,16,512]{2,1,0:T(8,128)S(1)}, f32[2,16,512]{2,1,0:T(8,128)}, u32[]{:S(2)}) %copy-start.11) | copy-done | bytes 65560
  13.0 0.0 copy-start.12
  13.0 0.8 %copy-done.12 = f32[2,16,256]{2,1,0:T(8,128)S(1)} copy-done((f32[2,16,256]{2,1,0:T(8,128)S(1)}, f32[2,16,256]{2,1,0:T(8,128)}, u32[]{:S(2)}) %copy-start.12) | copy-done | bytes 32792
  13.8 0.0 copy-start.13
  13.8 0.7 %copy-done.13 = f32[2,8,256]{2,1,0:T(8,128)S(1)} copy-done((f32[2,8,256]{2,1,0:T(8,128)S(1)}, f32[2,8,256]{2,1,0:T(8,128)}, u32[]{:S(2)}) %copy-start.13) | copy-done | bytes 16408
  14.5 0.0 copy-start.7
  14.5 46.3 %exchange.1.g_ref = f32[16,128,128]{2,1,0:T(8,128)S(1)} custom-call(f32[1]{0:T(128)S(6)} %copy.27.step_ref, f32[3,128,256]{2,1,0:T(8,128)S(1)} %bitcast.10, f32[3,128,256]{2,1,0:T(8,128)S(1)} %bitcast.12, bf16[2,2,2,32,1024]{4,3,2,1,0:T(8,128)(2,1)S(1)} %copy-done.3, f32[256,8]{1,0:T(8,128)S(1)} %copy.25.lift_ref, bf16[64,768]{1,0:T(8,128)(2,1)S(1)} %copy-done.9, ...), custom_call_target="tpu_custom_call" | custom-call | tf_op jit(solution)/shard_map/exchange/pallas_call | solution.py:358
  60.8 0.0 copy-done.7
  60.8 5.1 %cells.1 = bf16[32,8,16,256]{3,2,1,0:T(8,128)(2,1)} custom-call(f32[1]{0:T(128)S(6)} %copy.27.step_ref, f32[32,4]{1,0:T(8,128)S(1)} %fusion.local_ref, f32[16,128,128]{2,1,0:T(8,128)S(1)} %exchange.1.g_ref, f32[3,128,256]{2,1,0:T(8,128)S(1)} %bitcast.11, f32[3,128,256]{2,1,0:T(8,128)S(1)} %bitcast.13, bf16[384,512]{1,0:T(8,128)(2,1)S(1)} %copy-done.7), custom_call_target="tpu_custom_call" | custom-call | tf_op jit(solution)/shard_map/cells/pallas_call | solution.py:376
  (1 shorter events, 0.0 us)
Async XLA Ops:
  0.0 2.3 %copy-start = (f32[32,32]{1,0:T(8,128)S(1)}, f32[32,32]{1,0:T(8,128)}, u32[]{:S(2)}) copy-start(f32[32,32]{1,0:T(8,128)} %param.24) | copy-start | bytes 12292
  3.3 1.0 %copy-start.1 = (f32[1,3,8,16,256]{4,3,2,1,0:T(8,128)S(1)}, f32[1,3,8,16,256]{4,3,2,1,0:T(8,128)}, u32[]{:S(2)}) copy-start(f32[1,3,8,16,256]{4,3,2,1,0:T(8,128)} %param.18) | copy-start | bytes 1179652
  4.3 1.0 %copy-start.2 = (f32[1,3,8,16,256]{4,3,2,1,0:T(8,128)S(1)}, f32[1,3,8,16,256]{4,3,2,1,0:T(8,128)}, u32[]{:S(2)}) copy-start(f32[1,3,8,16,256]{4,3,2,1,0:T(8,128)} %param.19) | copy-start | bytes 1179652
  5.3 1.0 %copy-start.3 = (bf16[2,2,2,32,1024]{4,3,2,1,0:T(8,128)(2,1)S(1)}, bf16[2,2,2,32,1024]{4,3,2,1,0:T(8,128)(2,1)}, u32[]{:S(2)}) copy-start(bf16[2,2,2,32,1024]{4,3,2,1,0:T(8,128)(2,1)} %w_hbm.1) | copy-start | bytes 1572868
  6.3 1.0 %copy-start.4 = (bf16[2,512,256]{2,1,0:T(8,128)(2,1)S(1)}, bf16[2,512,256]{2,1,0:T(8,128)(2,1)}, u32[]{:S(2)}) copy-start(bf16[2,512,256]{2,1,0:T(8,128)(2,1)} %constant.30.clone.ey_hbm) | copy-start | bytes 1572868
  7.4 1.0 %copy-start.5 = (f32[2,128,512]{2,1,0:T(8,128)S(1)}, f32[2,128,512]{2,1,0:T(8,128)}, u32[]{:S(2)}) copy-start(f32[2,128,512]{2,1,0:T(8,128)} %constant.26.clone.bx_hbm) | copy-start | bytes 1572868
  8.4 1.0 %copy-start.6 = (bf16[2,256,512]{2,1,0:T(8,128)(2,1)S(1)}, bf16[2,256,512]{2,1,0:T(8,128)(2,1)}, u32[]{:S(2)}) copy-start(bf16[2,256,512]{2,1,0:T(8,128)(2,1)} %constant.24.clone.by_hbm) | copy-start | bytes 1572868
  9.5 0.9 %copy-start.8 = (bf16[1024,128]{1,0:T(8,128)(2,1)S(1)}, bf16[1024,128]{1,0:T(8,128)(2,1)}, u32[]{:S(2)}) copy-start(bf16[1024,128]{1,0:T(8,128)(2,1)} %constant.28.clone.sel_hbm) | copy-start | bytes 786436
  10.4 0.9 %copy-start.9 = (bf16[64,768]{1,0:T(8,128)(2,1)S(1)}, bf16[64,768]{1,0:T(8,128)(2,1)}, u32[]{:S(2)}) copy-start(bf16[64,768]{1,0:T(8,128)(2,1)} %constant.10.clone.fz_hbm) | copy-start | bytes 294916
  11.3 0.8 %copy-start.10 = (bf16[128,192]{1,0:T(8,128)(2,1)S(1)}, bf16[128,192]{1,0:T(8,128)(2,1)}, u32[]{:S(2)}) copy-start(bf16[128,192]{1,0:T(8,128)(2,1)} %constant.29.clone.ix_hbm) | copy-start | bytes 147460
  12.2 0.8 %copy-start.11 = (f32[2,16,512]{2,1,0:T(8,128)S(1)}, f32[2,16,512]{2,1,0:T(8,128)}, u32[]{:S(2)}) copy-start(f32[2,16,512]{2,1,0:T(8,128)} %constant.27.clone.twx_hbm) | copy-start | bytes 196612
  13.0 0.8 %copy-start.12 = (f32[2,16,256]{2,1,0:T(8,128)S(1)}, f32[2,16,256]{2,1,0:T(8,128)}, u32[]{:S(2)}) copy-start(f32[2,16,256]{2,1,0:T(8,128)} %constant.25.clone.twy_hbm) | copy-start | bytes 98308
  13.8 0.7 %copy-start.13 = (f32[2,8,256]{2,1,0:T(8,128)S(1)}, f32[2,8,256]{2,1,0:T(8,128)}, u32[]{:S(2)}) copy-start(f32[2,8,256]{2,1,0:T(8,128)} %constant.31.clone.twi_hbm) | copy-start | bytes 49156
  14.5 46.3 %copy-start.7 = (bf16[384,512]{1,0:T(8,128)(2,1)S(1)}, bf16[384,512]{1,0:T(8,128)(2,1)}, u32[]{:S(2)}) copy-start(bf16[384,512]{1,0:T(8,128)(2,1)} %constant.32.clone.iz_ref) | copy-start | bytes 1179652

commit v2 on v1

--- a/solution.py
+++ b/solution.py
@@ -12,6 +12,7 @@
 F32 = jnp.float32
 BF16 = jnp.bfloat16
 MESH = pl.DeviceIdType.MESH
+VMEM_LIMIT = 60 * 1024 * 1024
 N = 16
 
 
@@ -27,6 +28,10 @@
 
 def dot_nt(a, b):
     return lax.dot_general(a, b, (((1,), (1,)), ((), ())), preferred_element_type=F32)
+
+
+def dot_exact(a, b):
+    return jnp.dot(a, b, precision=lax.Precision.HIGHEST, preferred_element_type=F32)
 
 
 def np_split(x):
@@ -133,14 +138,32 @@
     return u[:32] + u[32:] + dot(hi, bx_lo)
 
 
+def lift_table(rows):
+    i = lax.broadcasted_iota(jnp.int32, (32, 128), 0)
+    lane = lax.broadcasted_iota(jnp.int32, (32, 128), 1)
+    wide = dot_exact(rows, jnp.where(lane % 32 == i, 1.0, 0.0).astype(F32))
+    upper = lax.broadcasted_iota(jnp.int32, (8, 128), 0) < 4
+    return jnp.concatenate([jnp.where(upper, wide, 0.0), jnp.where(upper, 0.0, wide)], 1)
+
+
+def local_table(rows, local_weight, local_bias):
+    wide = jnp.concatenate([jnp.broadcast_to(rows[j:j + 1], (128, 32)) for j in range(4)], 0)
+    scale = lax.dot_general(
+        local_weight, wide, (((1,), (1,)), ((), ())), precision=lax.Precision.HIGHEST,
+        preferred_element_type=F32)
+    same = lax.broadcasted_iota(jnp.int32, (32, 32), 0) == lax.broadcasted_iota(
+        jnp.int32, (32, 32), 1)
+    bias = lax.dot_general(
+        jnp.where(same, 1.0, 0.0).astype(F32), jnp.broadcast_to(local_bias, (128, 32)),
+        (((1,), (1,)), ((), ())), precision=lax.Precision.HIGHEST, preferred_element_type=F32)
+    return jnp.concatenate([scale[:, :384], scale[:, 384:] + bias], 1)
+
+
 def lifted_coeffs(total, first, lift):
     row = lax.broadcasted_iota(jnp.int32, (8, 128), 0)
     lane = lax.broadcasted_iota(jnp.int32, (8, 128), 1)
     total = total * (1.0 / 8388608.0) + jnp.where((row == 3) & (lane == 0), first, 0.0)
-    return lax.dot_general(
-        total.T, lift, (((1,), (1,)), ((), ())), precision=lax.Precision.HIGHEST,
-        preferred_element_type=F32,
-    )
+    return dot_exact(total.T, lift)
 
 
 def mix(coeffs, weight, sel):
@@ -196,24 +219,21 @@
 
 
 def exchange_kernel(
-    step_ref, v_hbm, t_hbm, w_hbm, lift_ref, fz_hbm, by_hbm, twy_hbm, bx_hbm, twx_hbm, sel_hbm,
-    ix_hbm, ey_hbm, twi_hbm,
-    out_ref,
-    v_ref, t_ref, w_ref, fz_ref, by_ref, twy_ref, bx_ref, twx_ref, sel_ref, ix_ref, ey_ref, twi_ref,
-    s1, r1, s2, r2, s3, r3, s4,
-    load_sem, send1, recv1, send2, recv2, send3, recv3, send4, recv4,
+    *refs,
 ):
+    hbm, refs = refs[:17], refs[17:]
+    (out_ref, local_ref, adv_ref), refs = refs[:3], refs[3:]
+    local, refs = refs[:17], refs[17:]
+    (step_ref, v_ref, t_ref, fz_ref, by_ref, twy_ref, bx_ref, twx_ref, lift_ref, bias_ref, w_ref,
+     sel_ref, ix_ref, ey_ref, twi_ref, lw_ref, lb_ref) = local
+    (s1, r1, s2, r2, s3, r3, s4, rows_ref,
+     load_sem, send1, recv1, send2, recv2, send3, recv3, send4, recv4) = refs
     r = lax.axis_index("row")
     c = lax.axis_index("col")
 
     barrier = pltpu.get_barrier_semaphore()
-    pairs = [
-        (v_hbm, v_ref), (t_hbm, t_ref), (fz_hbm, fz_ref), (by_hbm, by_ref), (twy_hbm, twy_ref),
-        (bx_hbm, bx_ref), (twx_hbm, twx_ref), (w_hbm, w_ref), (sel_hbm, sel_ref), (ix_hbm, ix_ref),
-        (ey_hbm, ey_ref), (twi_hbm, twi_ref),
-    ]
     loads = [
-        pltpu.make_async_copy(src, dst, load_sem.at[n]) for n, (src, dst) in enumerate(pairs)
+        pltpu.make_async_copy(src, dst, load_sem.at[n]) for n, (src, dst) in enumerate(zip(hbm, local))
     ]
     for load in loads:
         load.start()
@@ -223,9 +243,11 @@
         pl.semaphore_signal(
             barrier, inc=1, device_id={"row": (r + d) % N, "col": c}, device_id_type=MESH)
 
-    for load in loads[:3]:
+    for load in loads[:4]:
         load.wait()
-    advanced = (v_ref[...] + step_ref[0] * t_ref[...]).reshape(384, 256)
+    advanced = v_ref[...] + step_ref[0] * t_ref[...]
+    adv_ref[...] = advanced
+    advanced = advanced.reshape(384, 256)
     z = forward_z(advanced, fz_ref[...])
     s1[pl.ds(3, 64, stride=4), :] = jnp.zeros((64, 128), F32)
     for j in range(3):
@@ -252,10 +274,15 @@
             first[-1].start()
     for part in range(2):
         r1[part, c] = s1[pl.ds(pl.multiple_of(128 * part + 8 * c, 8), 8), :]
-    for load in loads[3:]:
+    for load in loads[4:]:
         load.wait()
     bx_hi, bx_lo = x_table(
         bx_ref[0], bx_ref[1], twx_ref[0, pl.ds(r, 1), :], twx_ref[1, pl.ds(r, 1), :])
+    for k in (0, 4):
+        rows_ref[k:k + 3] = lift_ref[...]
+        rows_ref[k + 3:k + 4] = bias_ref[...]
+    lift = lift_table(rows_ref[...])
+    local_ref[...] = local_table(rows_ref[...], lw_ref[...], lb_ref[...])
     for copy in first:
         copy.wait_recv()
 
@@ -276,7 +303,7 @@
     total = jnp.sum(r2[...], axis=0)
 
     origin = jnp.where((r == 0) & (c == 0), 1.0, 0.0).astype(F32)
-    coeffs = lifted_coeffs(total, origin, lift_ref[...])
+    coeffs = lifted_coeffs(total, origin, lift)
     mixed = mix(coeffs, lambda part, ky, kz: w_ref[part, ky, kz], sel_ref[...])
     for ky in range(2):
         s3[:, 8 * ky:8 * ky + 8, :] = inverse_x(mixed, ky, ix_ref[...]).reshape(16, 8, 128)
@@ -315,17 +342,15 @@
         copy.wait_send()
 
 
-def cells_kernel(step_ref, local_ref, g_ref, v_ref, t_ref, iz_ref, out_ref, adv_ref):
-    @pl.when(pl.program_id(0) == 0)
-    def _():
-        adv_ref[...] = v_ref[...] + step_ref[0] * t_ref[...]
-
-    base = pl.program_id(0) * 8
+def cells_kernel(local_ref, g_ref, adv_ref, iz_ref, out_ref):
     for q in range(4):
         values = inverse_z(g_ref[:, 8 * q:8 * q + 8, :].reshape(128, 128), iz_ref[...])
         for o in range(2):
-            index = base + 2 * q + o
-            scale = [local_ref[index, j] for j in range(4)]
+            index = 2 * q + o
+            scale = [
+                jnp.concatenate([local_ref[index:index + 1, 128 * j:128 * j + 128]] * 2, 1)
+                for j in range(4)
+            ]
             for x in range(8):
                 cell = slice(16 * x, 16 * x + 16)
                 value = values[cell, 256 * o:256 * o + 256] + scale[3]
@@ -337,58 +362,52 @@
 def per_device(
     velocity, tendency, step_size, lift_weight, lift_bias, spectral_weight, local_weight, local_bias
 ):
-    highest = lax.Precision.HIGHEST
     t = tables()
     v = velocity.reshape(3, 128, 256)
     dv = tendency.reshape(3, 128, 256)
-    four = jnp.concatenate([lift_weight, lift_bias[:, None]], 1)
-    four = jnp.concatenate([four] * 4, 0)
-    zero = jnp.zeros((128, 4), F32)
-    lift = jnp.concatenate(
-        [jnp.concatenate([four, zero], 1), jnp.concatenate([zero, four], 1)], 0)
-    local = jnp.dot(local_weight, four[:32], precision=highest)
-    local = local + jnp.concatenate([jnp.zeros((32, 3), F32), local_bias[:, None]], 1)
-
     vmem = pl.BlockSpec(memory_space=pltpu.VMEM)
-    smem = pl.BlockSpec(memory_space=pltpu.SMEM)
     anywhere = pl.BlockSpec(memory_space=pl.ANY)
-    far = [v, dv, spectral_weight]
-    consts = [t[n] for n in ("fwd_z", "by", "tw_y", "bx", "tw_x", "sel", "inv_x", "ey", "tw_i")]
-    scratch = [pltpu.VMEM(a.shape, a.dtype) for a in far + consts]
-    blocks = pl.pallas_call(
+    const = {name: jnp.asarray(a) for name, a in t.items()}
+    far = [
+        step_size, v, dv, const["fwd_z"], const["by"], const["tw_y"], const["bx"], const["tw_x"],
+        lift_weight.T, lift_bias[None, :], spectral_weight, const["sel"], const["inv_x"],
+        const["ey"], const["tw_i"], local_weight, local_bias[None, :],
+    ]
+    scratch = [pltpu.SMEM((1,), F32)] + [pltpu.VMEM(a.shape, a.dtype) for a in far[1:]]
+    blocks, local, advanced = pl.pallas_call(
         exchange_kernel,
-        out_shape=jax.ShapeDtypeStruct((16, 128, 128), F32),
-        in_specs=[smem] + [anywhere] * 3 + [vmem] + [anywhere] * len(consts),
-        out_specs=vmem,
+        out_shape=(
+            jax.ShapeDtypeStruct((16, 128, 128), F32), jax.ShapeDtypeStruct((32, 512), F32),
+            jax.ShapeDtypeStruct((3, 128, 256), F32)),
+        in_specs=[anywhere] * len(far),
+        out_specs=(vmem, vmem, vmem),
         scratch_shapes=scratch + [
             pltpu.VMEM((256, 128), F32), pltpu.VMEM((2, 16, 8, 128), F32),
             pltpu.VMEM((16, 8, 128), F32), pltpu.VMEM((16, 8, 128), F32),
             pltpu.VMEM((16, 16, 128), F32), pltpu.VMEM((16, 16, 128), F32),
-            pltpu.VMEM((16, 128, 128), F32),
-            pltpu.SemaphoreType.DMA((12,)),
+            pltpu.VMEM((16, 128, 128), F32), pltpu.VMEM((8, 32), F32),
+            pltpu.SemaphoreType.DMA((len(far),)),
             pltpu.SemaphoreType.DMA((2, 16)), pltpu.SemaphoreType.DMA((2, 16)),
         ] + [pltpu.SemaphoreType.DMA((16,))] * 6,
         compiler_params=pltpu.CompilerParams(
-            collective_id=0, has_side_effects=True, vmem_limit_bytes=40 * 1024 * 1024),
+            collective_id=0, has_side_effects=True, vmem_limit_bytes=VMEM_LIMIT),
         name="exchange",
-    )(step_size, *far, lift, *[jnp.asarray(a) for a in consts])
+    )(*far)
 
     out = pl.pallas_call(
         cells_kernel,
         grid=(4,),
         out_shape=jax.ShapeDtypeStruct((32, 8, 16, 256), BF16),
         in_specs=[
-            smem, smem,
+            pl.BlockSpec((8, 512), lambda i: (i, 0)),
             pl.BlockSpec((16, 32, 128), lambda i: (0, i, 0)),
-            pl.BlockSpec((3, 128, 256), lambda i: (0, 0, 0)),
             pl.BlockSpec((3, 128, 256), lambda i: (0, 0, 0)),
             pl.BlockSpec((384, 512), lambda i: (0, 0)),
         ],
         out_specs=pl.BlockSpec((8, 8, 16, 256), lambda i: (i, 0, 0, 0)),
-        scratch_shapes=[pltpu.VMEM((3, 128, 256), F32)],
-        compiler_params=pltpu.CompilerParams(vmem_limit_bytes=40 * 1024 * 1024),
+        compiler_params=pltpu.CompilerParams(vmem_limit_bytes=VMEM_LIMIT),
         name="cells",
-    )(step_size, local, blocks, v, dv, jnp.asarray(t["inv_z"]))
+    )(local, blocks, advanced, const["inv_z"])
     return out.reshape(1, 32, 8, 16, 256)
 
 

time: 66.6 us -> 53.3 us (0.80)
  local copies, waits for them, and re-layouts: 12 us -> 0 us
  Pallas kernels: 51.4 us -> 52.5 us
  other arithmetic: 0.92 us -> 0 us
  matrix products: 0.84 us -> 0 us
    unnamed x28 -> x0, local copies, waits for them, and re-layouts: 11.2 us -> none
    concatenate x2 -> x0, other arithmetic: 0.92 us -> none  [the longest x1 0.91 us: per_device(): four = jnp.concatenate([four] * 4, 0)]
    dot_general x1 -> x0, matrix products: 0.84 us -> none  [per_device(): local = jnp.dot(local_weight, four[:32], precision=highest)]
    broadcast_in_dim x1 -> x0, local copies, waits for them, and re-layouts: 0.74 us -> none  [per_device(): local_bias[:, None]]
where the time goes in v2:
time: 53.3 us; the launch traced here: 53.1 us
  Pallas kernels  52.5 us (98%)
  between operations  0.66 us (1%)
    pallas_call x1, Pallas kernels, per_device(): pl.pallas_call(exchange_kernel, out_shape=(jax.ShapeDtypeStruct((16, 128,...  46.8 us
    pallas_call x1, Pallas kernels, per_device(): pl.pallas_call(cells_kernel, grid=(4,), out_shape=jax.ShapeDtypeStruct((3...  5.69 us

profile of v2, /device:TPU:1, one launch (start us, length us, event | category | flops | bytes accessed | tf_op | source)
XLA Modules:
  0.0 53.1 jit_solution(10550135297398499192)
XLA Ops:
  0.7 46.8 %exchange.1 = (f32[16,128,128]{2,1,0:T(8,128)}, f32[32,512]{1,0:T(8,128)}, f32[3,128,256]{2,1,0:T(8,128)}) custom-call(f32[1]{0:T(128)S(6)} %copy.19.refs_0_, f32[3,128,256]{2,1,0:T(8,128)} %bitcast.6, f32[3,128,256]{2,1,0:T(8,128)} %bitcast.7, bf16[64,768]{1,0:T(8,128)(2,1)} %constant.20.clone.refs_3_, bf16[2,256,512]{2,1,0:T(8,128)(2,1)} %constant.21.clone.refs_4_, ...), custom_call_target="tpu_custom_call" | custom-call | tf_op jit(solution)/shard_map/exchange/pallas_call | solution.py:377
  47.4 5.7 %cells.1 = bf16[32,8,16,256]{3,2,1,0:T(8,128)(2,1)} custom-call(f32[32,512]{1,0:T(8,128)} %get-tuple-element.8.local_ref, f32[16,128,128]{2,1,0:T(8,128)} %get-tuple-element.9.g_ref, f32[3,128,256]{2,1,0:T(8,128)} %get-tuple-element.10.adv_ref, bf16[384,512]{1,0:T(8,128)(2,1)} %constant.29.clone.iz_ref), custom_call_target="tpu_custom_call" | custom-call | tf_op jit(solution)/shard_map/cells/pallas_call | solution.py:397

commit v3 on v2

v3 whole, which is shorter than its diff:
```python
import functools
import math

import jax
import jax.numpy as jnp
import numpy as np
from jax import lax
from jax.experimental import pallas as pl
from jax.experimental.pallas import tpu as pltpu
from jax.sharding import PartitionSpec as P

F32 = jnp.float32
BF16 = jnp.bfloat16
MESH = pl.DeviceIdType.MESH
VMEM_LIMIT = 60 * 1024 * 1024
N = 16


def split(x):
    hi = x.astype(BF16)
    lo = (x - hi.astype(F32)).astype(BF16)
    return hi, lo


def dot(a, b):
    return jnp.dot(a, b, preferred_element_type=F32)


def dot_nt(a, b):
    return lax.dot_general(a, b, (((1,), (1,)), ((), ())), preferred_element_type=F32)


def dot_exact(a, b):
    return jnp.dot(a, b, precision=lax.Precision.HIGHEST, preferred_element_type=F32)


def np_split(x):
    x = np.asarray(x, np.float64)
    hi = x.astype(np.float32).astype(jnp.bfloat16)
    lo = (x - hi.astype(np.float64)).astype(np.float32).astype(jnp.bfloat16)
    return hi, lo


@functools.lru_cache(None)
def tables():
    turn = 2.0 * np.pi
    ix = np.arange
    waves = np.where(ix(32) < 16, ix(32), ix(32) - 32)
    eye8 = np.eye(8)
    z_angle = turn * (ix(32)[:, None] * ix(256)[None, :] % 256) / 256
    z_hi, z_lo = np_split(np.concatenate([np.cos(z_angle), -np.sin(z_angle)], 0))
    fwd_z = np.concatenate([z_hi, z_lo, z_hi], 1)
    fwd_z = fwd_z.reshape(2, 16, 2, 768).transpose(1, 0, 2, 3).reshape(64, 768)
    a = turn * waves[None, :] * ix(16)[:, None] / 256
    by = np.zeros((2, 8, 16, 2, 32, 8))
    for x in range(8):
        by[0, x, :, 0, :, x] = np.cos(a)
        by[1, x, :, 0, :, x] = np.sin(a)
        by[0, x, :, 1, :, x] = -np.sin(a)
        by[1, x, :, 1, :, x] = np.cos(a)
    by_hi, by_lo = np_split(by.reshape(256, 512))
    b = turn * (waves[None, :] * ix(16)[:, None] % 16) / 16
    b = np.repeat(b, 8, axis=1)
    tw_y = np.stack([np.cos(b), np.sin(b)], 0).astype(np.float32)
    c = turn * waves[None, :] * ix(8)[:, None] / 128
    bx = []
    for quarter in (0.0, np.pi / 2):
        t = np.zeros((2, 8, 8, 8, 2, 32))
        for e in range(8):
            t[0, e, :, e, 0, :] = np.cos(c + quarter)
            t[1, e, :, e, 0, :] = np.sin(c + quarter)
            t[0, e, :, e, 1, :] = -np.sin(c + quarter)
            t[1, e, :, e, 1, :] = np.cos(c + quarter)
        bx.append(t.reshape(128, 512))
    bx = np.stack(bx, 0).astype(np.float32)
    d = turn * (waves[None, :] * ix(16)[:, None] % 16) / 16
    d = np.tile(d, (1, 16))
    tw_x = np.stack([np.cos(d), np.sin(d)], 0).astype(np.float32)
    sel = (ix(512)[:, None] // 32 == ix(128)[None, :] // 4 % 16).astype(jnp.bfloat16)
    f = turn * (waves[None, :] * ix(128)[:, None] % 128) / 128
    ex_hi, ex_lo = np_split(np.concatenate([np.cos(f), np.sin(f)], 1))
    inv_x = np.concatenate([ex_hi, ex_hi, ex_lo], 1)
    g = turn * waves[:, None] * ix(32)[None, :] / 256
    ey = np.zeros((2, 32, 8, 2, 8, 16))
    for x in range(8):
        for blk in range(2):
            ey[0, :, x, blk, x, :] = np.cos(g[:, blk * 16:blk * 16 + 16])
            ey[1, :, x, blk, x, :] = -np.sin(g[:, blk * 16:blk * 16 + 16])
    ey = ey.reshape(2, 16, 2, 8, 256).transpose(0, 2, 1, 3, 4)
    ey_hi, ey_lo = np_split(ey.reshape(512, 256))
    h = turn * (waves[None, :] * ix(8)[:, None] % 8) / 8
    h = np.repeat(h.reshape(8, 16, 2).transpose(0, 2, 1).reshape(8, 32), 8, axis=1)
    tw_i = np.stack([np.cos(h), np.sin(h)], 0).astype(np.float32)
    ez = np.zeros((16, 2, 2, 2, 2, 256))
    weight = np.where(ix(32) == 0, 1.0, 2.0)[:, None]
    cz = (weight * np.cos(z_angle)).reshape(16, 2, 256)
    sz = (-weight * np.sin(z_angle)).reshape(16, 2, 256)
    for o in range(2):
        ez[:, o, :, 0, o, :] = cz
        ez[:, o, :, 1, o, :] = sz
    ez_hi, ez_lo = np_split(ez.reshape(128, 512))
    inv_z = np.concatenate([ez_hi, ez_hi, ez_lo], 0)
    return dict(
        fwd_z=fwd_z, by=np.stack([by_hi, by_lo], 0), tw_y=tw_y, bx=bx, tw_x=tw_x, sel=sel,
        inv_x=inv_x, ey=np.stack([ey_hi, ey_lo], 0), tw_i=tw_i, inv_z=inv_z,
    )


def forward_z(advanced, fwd_z):
    hi, lo = split(advanced)
    return dot_nt(fwd_z, jnp.concatenate([hi, hi, lo], 1))


def forward_y(arrived, by_hi, by_lo, tw_c, tw_s):
    hi, lo = split(arrived)
    u = dot(jnp.concatenate([hi, lo], 0), by_hi)
    u = u[:128] + u[128:] + dot(hi, by_lo)
    real, imag = jnp.zeros((8, 256), F32), jnp.zeros((8, 256), F32)
    for c in range(N):
        ur, ui = u[8 * c:8 * c + 8, :256], u[8 * c:8 * c + 8, 256:]
        tc, ts = tw_c[c:c + 1, :], tw_s[c:c + 1, :]
        real += ur * tc + ui * ts
        imag += ui * tc - ur * ts
    return real, imag


def x_table(bx0, bx1, tc, ts):
    return split(bx0 * tc + bx1 * ts)


def forward_x(real, imag, bx_hi, bx_lo, roll):
    low = lax.broadcasted_iota(jnp.int32, (8, 128), 1) < 64
    rows = []
    for v in range(2):
        re, im = real[:, 128 * v:128 * v + 128], imag[:, 128 * v:128 * v + 128]
        rows.append(jnp.where(low, re, roll(im, 64, 1)))
        rows.append(jnp.where(low, roll(re, 64, 1), im))
    hi, lo = split(jnp.concatenate(rows, 0))
    u = dot(jnp.concatenate([hi, lo], 0), bx_hi)
    return u[:32] + u[32:] + dot(hi, bx_lo)


def lift_table(rows):
    i = lax.broadcasted_iota(jnp.int32, (32, 128), 0)
    lane = lax.broadcasted_iota(jnp.int32, (32, 128), 1)
    wide = dot_exact(rows, jnp.where(lane % 32 == i, 1.0, 0.0).astype(F32))
    upper = lax.broadcasted_iota(jnp.int32, (8, 128), 0) < 4
    return jnp.concatenate([jnp.where(upper, wide, 0.0), jnp.where(upper, 0.0, wide)], 1)


def local_table(rows, local_weight, local_bias):
    wide = jnp.concatenate([jnp.broadcast_to(rows[j:j + 1], (128, 32)) for j in range(4)], 0)
    scale = lax.dot_general(
        local_weight, wide, (((1,), (1,)), ((), ())), precision=lax.Precision.HIGHEST,
        preferred_element_type=F32)
    same = lax.broadcasted_iota(jnp.int32, (32, 32), 0) == lax.broadcasted_iota(
        jnp.int32, (32, 32), 1)
    bias = lax.dot_general(
        jnp.where(same, 1.0, 0.0).astype(F32), jnp.broadcast_to(local_bias, (128, 32)),
        (((1,), (1,)), ((), ())), precision=lax.Precision.HIGHEST, preferred_element_type=F32)
    return jnp.concatenate([scale[:, :384], scale[:, 384:] + bias], 1)


def lifted_coeffs(total, first, lift):
    row = lax.broadcasted_iota(jnp.int32, (8, 128), 0)
    lane = lax.broadcasted_iota(jnp.int32, (8, 128), 1)
    total = total * (1.0 / 8388608.0) + jnp.where((row == 3) & (lane == 0), first, 0.0)
    return dot_exact(total.T, lift)


def mix(coeffs, weight, sel):
    his, los = [], []
    for ky in range(2):
        for kz in range(2):
            cr = coeffs[64 * ky:64 * ky + 32, 128 * kz:128 * kz + 128]
            ci = coeffs[64 * ky + 32:64 * ky + 64, 128 * kz:128 * kz + 128]
            cr4 = jnp.concatenate([cr] * 4, 1)
            ci4 = jnp.concatenate([ci] * 4, 1)
            wr = weight(0, ky, kz).astype(F32)
            wi = weight(1, ky, kz).astype(F32)
            for value in (wr * cr4 - wi * ci4, wr * ci4 + wi * cr4):
                hi, lo = split(value)
                his.append(hi)
                los.append(lo)
    return dot(jnp.concatenate(his, 0), sel) + dot(jnp.concatenate(los, 0), sel)


def inverse_x(mixed, inv_x):
    lane = lax.broadcasted_iota(jnp.int32, (32, 128), 1)
    kind = lane % 4
    tops, bottoms = [], []
    for ky in range(2):
        block = [mixed[128 * ky + 32 * n:128 * ky + 32 * n + 32] for n in range(4)]

        def pick(a, b, c, d):
            return jnp.where(kind == 0, a, jnp.where(kind == 1, b, jnp.where(kind == 2, c, d)))

        tops.append(pick(block[0], block[1], block[2], block[3]))
        bottoms.append(pick(-block[1], block[0], -block[3], block[2]))
    top = jnp.where(lane < 64, tops[0], tops[1])
    bottom = jnp.where(lane < 64, bottoms[0], bottoms[1])
    hi, lo = split(jnp.concatenate([top, bottom], 0))
    return dot(inv_x, jnp.concatenate([hi, lo, hi], 0))


def turned(arrived, roll):
    even = lax.broadcasted_iota(jnp.int32, arrived.shape, 1) % 2 == 0
    other = jnp.where(even, roll(arrived, 127, 1), -roll(arrived, 1, 1))
    return [jnp.concatenate([t[:64], t[64:]], 1) for t in (arrived.T, other.T)]


def inverse_y(plain, other, tw_c, tw_s, ey_hi, ey_lo):
    his, los = [], []
    for m in range(8):
        tc, ts = tw_c[m:m + 1, :], tw_s[m:m + 1, :]
        hi, lo = split(jnp.concatenate([plain * tc - other * ts, other * tc + plain * ts], 1))
        his.append(hi)
        los.append(lo)
    hi, lo = jnp.concatenate(his, 0), jnp.concatenate(los, 0)
    return dot(hi, ey_hi) + dot(lo, ey_hi) + dot(hi, ey_lo)


def inverse_z(block, inv_z):
    hi, lo = split(block.T)
    return dot(jnp.concatenate([hi, lo, hi], 1), inv_z)


def activate(value):
    cubic = value * (0.7978845608028654 + 0.035677408136300125 * (value * value))
    half = 0.5 * value
    return half + half * jnp.tanh(cubic)


def ring(step, length):
    return min(step, length - step)


ROW_STEPS = sorted(
    ((a, b) for a in range(8) for b in range(2) if a or b), key=lambda s: (-ring(s[0], 8), s))
COL_STEPS = sorted(
    ((a, b) for a in range(4) for b in range(4) if a or b),
    key=lambda s: (-ring(s[0], 4) - ring(s[1], 4), s))
PIECES = ((0, 8), (8, 8), (16, 8), (24, 8))


def layer_kernel(*refs):
    hbm, refs = refs[:18], refs[18:]
    out_ref, refs = refs[0], refs[1:]
    here, refs = refs[:18], refs[18:]
    (step_ref, v_ref, t_ref, fz_ref, by_ref, twy_ref, bx_ref, twx_ref, lift_ref, bias_ref, lw_ref,
     lb_ref, w_ref, sel_ref, ix_ref, ey_ref, twi_ref, iz_ref) = here
    (adv_ref, local_ref, s1, r1, s2, r2, s3, r3, s4, g_ref, rows_ref,
     load_sem, send1, recv1, send2, recv2, send3, recv3, send4, recv4) = refs
    r = lax.axis_index("row")
    c = lax.axis_index("col")
    row_peers = [((r // 2 + a) % 8) * 2 + (r + b) % 2 for a, b in ROW_STEPS]
    col_peers = [((c // 4 + a) % 4) * 4 + (c + b) % 4 for a, b in COL_STEPS]

    loads = [
        pltpu.make_async_copy(src, dst, load_sem.at[n]) for n, (src, dst) in enumerate(zip(hbm, here))
    ]
    for load in loads[:4]:
        load.start()
    barrier = pltpu.get_barrier_semaphore()
    for peer in col_peers:
        pl.semaphore_signal(
            barrier, inc=1, device_id={"row": r, "col": peer}, device_id_type=MESH)
    for peer in row_peers:
        pl.semaphore_signal(
            barrier, inc=1, device_id={"row": peer, "col": c}, device_id_type=MESH)
    for load in loads[4:]:
        load.start()

    def to_col(src, dst, send, recv, peer):
        copy = pltpu.make_async_remote_copy(
            src_ref=src, dst_ref=dst, send_sem=send, recv_sem=recv,
            device_id={"row": r, "col": peer}, device_id_type=MESH)
        copy.start()
        return copy

    def to_row(src, dst, send, recv, peer):
        copy = pltpu.make_async_remote_copy(
            src_ref=src, dst_ref=dst, send_sem=send, recv_sem=recv,
            device_id={"row": peer, "col": c}, device_id_type=MESH)
        copy.start()
        return copy

    for load in loads[:4]:
        load.wait()
    advanced = v_ref[...] + step_ref[0] * t_ref[...]
    adv_ref[...] = advanced
    z = forward_z(advanced.reshape(384, 256), fz_ref[...])
    s1[pl.ds(3, 64, stride=4), :] = jnp.zeros((64, 128), F32)
    for j in range(3):
        s1[pl.ds(j, 64, stride=4), :] = z[:, 128 * j:128 * j + 128]
    pl.semaphore_wait(barrier, 2 * (N - 1))
    first = [
        to_col(s1.at[pl.ds(pl.multiple_of(16 * peer, 16), 16)], r1.at[c], send1.at[k], recv1.at[k],
               peer)
        for k, peer in enumerate(col_peers)
    ]
    r1[c] = s1[pl.ds(pl.multiple_of(16 * c, 16), 16), :]
    for load in loads[4:]:
        load.wait()
    bx_hi, bx_lo = x_table(
        bx_ref[0], bx_ref[1], twx_ref[0, pl.ds(r, 1), :], twx_ref[1, pl.ds(r, 1), :])
    for k in (0, 4):
        rows_ref[k:k + 3] = lift_ref[...]
        rows_ref[k + 3:k + 4] = bias_ref[...]
    lift = lift_table(rows_ref[...])
    local_ref[...] = local_table(rows_ref[...], lw_ref[...], lb_ref[...])
    for copy in first:
        copy.wait_recv()

    arrived = jnp.concatenate(
        [r1[:, 8 * part:8 * part + 8, :].reshape(128, 128) for part in range(2)], 1)
    real, imag = forward_y(arrived, by_ref[0], by_ref[1], twy_ref[0], twy_ref[1])
    partial = forward_x(real, imag, bx_hi, bx_lo, pltpu.roll)
    for g in range(4):
        for k in range(4):
            s2[4 * g + k] = partial[8 * g:8 * g + 8, 128 * k:128 * k + 128]
    second = [
        to_row(s2.at[peer], r2.at[r], send2.at[k], recv2.at[k], peer)
        for k, peer in enumerate(row_peers)
    ]
    r2[r] = s2[r]
    for copy in second:
        copy.wait_recv()
    total = jnp.sum(r2[...], axis=0)

    origin = jnp.where((r == 0) & (c == 0), 1.0, 0.0).astype(F32)
    coeffs = lifted_coeffs(total, origin, lift)
    third = []
    for half in range(2):
        mixed = mix(
            coeffs,
            lambda part, ky, kz: w_ref[part, ky, kz, :, 512 * half:512 * half + 512],
            sel_ref[...])
        s3[half] = inverse_x(mixed, ix_ref[...]).reshape(16, 8, 128)
        third.append([
            to_row(s3.at[half, peer], r3.at[half, r], send3.at[half, k], recv3.at[half, k], peer)
            for k, peer in enumerate(row_peers)
        ])
        r3[half, r] = s3[half, r]

    fourth = []
    for piece, (start, count) in enumerate(PIECES):
        if start % 16 == 0:
            half = start // 16
            for copy in third[half]:
                copy.wait_recv()
            plain, other = turned(r3[half].reshape(128, 128), pltpu.roll)
        rows = 4 * count
        first_row = 4 * (start % 16)
        h = inverse_y(
            plain[first_row:first_row + rows], other[first_row:first_row + rows],
            twi_ref[0], twi_ref[1], ey_ref[0], ey_ref[1])
        span = pl.ds(4 * start, rows)
        for dest in range(N):
            m, b = dest // 2, dest % 2
            s4[dest, span, :] = h[rows * m:rows * m + rows, 128 * b:128 * b + 128]
        fourth.append([
            to_col(s4.at[peer, span], g_ref.at[c, span], send4.at[piece, k], recv4.at[piece, k],
                   peer)
            for k, peer in enumerate(col_peers)
        ])
        g_ref[c, span, :] = s4[c, span, :]

    for piece, (start, count) in enumerate(PIECES):
        for copy in fourth[piece]:
            copy.wait_recv()
        for o in range(start, start + count, 2):
            values = inverse_z(g_ref[:, 4 * o:4 * o + 8, :].reshape(128, 128), iz_ref[...])
            for k in range(2):
                scale = [
                    jnp.concatenate([local_ref[o + k:o + k + 1, 128 * j:128 * j + 128]] * 2, 1)
                    for j in range(4)
                ]
                for x in range(8):
                    cell = slice(16 * x, 16 * x + 16)
                    value = values[cell, 256 * k:256 * k + 256] + scale[3]
                    for j in range(3):
                        value += scale[j] * adv_ref[j, cell, :]
                    out_ref[o + k, x] = activate(value).astype(BF16)
    for copies in [first, second] + third + fourth:
        for copy in copies:
            copy.wait_send()


def per_device(
    velocity, tendency, step_size, lift_weight, lift_bias, spectral_weight, local_weight, local_bias
):
    const = {name: jnp.asarray(a) for name, a in tables().items()}
    far = [
        step_size, velocity.reshape(3, 128, 256), tendency.reshape(3, 128, 256), const["fwd_z"],
        const["by"], const["tw_y"], const["bx"], const["tw_x"], lift_weight.T, lift_bias[None, :],
        local_weight, local_bias[None, :], spectral_weight, const["sel"], const["inv_x"],
        const["ey"], const["tw_i"], const["inv_z"],
    ]
    dma = pltpu.SemaphoreType.DMA
    out = pl.pallas_call(
        layer_kernel,
        out_shape=pltpu.VMEM((32, 8, 16, 256), BF16),
        in_specs=[pl.BlockSpec(memory_space=pl.ANY)] * len(far),
        out_specs=pl.BlockSpec(memory_space=pltpu.VMEM),
        scratch_shapes=[pltpu.SMEM((1,), F32)] + [pltpu.VMEM(a.shape, a.dtype) for a in far[1:]] + [
            pltpu.VMEM((3, 128, 256), F32), pltpu.VMEM((32, 512), F32),
            pltpu.VMEM((256, 128), F32), pltpu.VMEM((16, 16, 128), F32),
            pltpu.VMEM((16, 8, 128), F32), pltpu.VMEM((16, 8, 128), F32),
            pltpu.VMEM((2, 16, 8, 128), F32), pltpu.VMEM((2, 16, 8, 128), F32),
            pltpu.VMEM((16, 128, 128), F32), pltpu.VMEM((16, 128, 128), F32),
            pltpu.VMEM((8, 32), F32),
            dma((len(far),)), dma((N,)), dma((N,)), dma((N,)), dma((N,)),
            dma((2, N)), dma((2, N)), dma((len(PIECES), N)), dma((len(PIECES), N)),
        ],
        compiler_params=pltpu.CompilerParams(
            collective_id=0, has_side_effects=True, vmem_limit_bytes=VMEM_LIMIT),
        name="layer",
    )(*far)
    return out.reshape(1, 32, 8, 16, 256)


def solution(mesh):
    in_specs = (
        P(None, None, "row", "col", None),
        P(None, None, "row", "col", None),
        P(),
        P(),
        P(),
        P(None, "row", "col", None, None),
        P(),
        P(),
    )
    out_specs = P(None, None, "row", "col", None)
    return jax.shard_map(
        per_device, mesh=mesh, in_specs=in_specs, out_specs=out_specs, check_vma=False
    )
```

time: 53.3 us -> 47 us (0.88)
  Pallas kernels: 52.5 us -> 45 us
  local copies, waits for them, and re-layouts: 0 us -> 1.32 us
    pallas_call x2 -> x1, Pallas kernels: 52.5 us -> 45 us  [per_device(): pl.pallas_call(layer_kernel, out_shape=pltpu.VMEM((32, 8, 16, 256), BF16)...]
    unnamed x0 -> x1, local copies, waits for them, and re-layouts: none -> 1.32 us
where the time goes in v3:
time: 47 us; the launch traced here: 46.9 us
  Pallas kernels  45 us (96%)
  local copies, waits for them, and re-layouts  1.32 us (3%)
  between operations  0.66 us (1%)
    pallas_call x1, Pallas kernels, per_device(): pl.pallas_call(layer_kernel, out_shape=pltpu.VMEM((32, 8, 16, 256), BF16)...  45 us
    unnamed x1, local copies, waits for them, and re-layouts  1.32 us

profile of v3, /device:TPU:1, one launch (start us, length us, event | category | flops | bytes accessed | tf_op | source)
XLA Modules:
  0.0 46.9 jit_solution(12697990879420394453)
XLA Ops:
  0.7 45.0 %layer.1 = bf16[32,8,16,256]{3,2,1,0:T(8,128)(2,1)S(1)} custom-call(f32[1]{0:T(128)S(6)} %copy.21.refs_0_, f32[3,128,256]{2,1,0:T(8,128)} %bitcast.7, f32[3,128,256]{2,1,0:T(8,128)} %bitcast.8, bf16[64,768]{1,0:T(8,128)(2,1)} %constant.20.clone.refs_3_, bf16[2,256,512]{2,1,0:T(8,128)(2,1)} %constant.21.clone.refs_4_, f32[2,16,256]{2,1,0:T(8,128)} %constant.22.clone.refs_5_, ...), custom_call_target="tpu_custom_call" | custom-call | tf_op jit(solution)/shard_map/layer/pallas_call | solution.py:401
  45.6 1.3 %copy.20 = bf16[1,32,8,16,256]{4,3,2,1,0:T(8,128)(2,1)} copy(bf16[1,32,8,16,256]{4,3,2,1,0:T(8,128)(2,1)S(1)} %bitcast.6) | data formatting | bytes 4194304

commit v4 on v3

--- a/solution.py
+++ b/solution.py
@@ -80,16 +80,19 @@
     f = turn * (waves[None, :] * ix(128)[:, None] % 128) / 128
     ex_hi, ex_lo = np_split(np.concatenate([np.cos(f), np.sin(f)], 1))
     inv_x = np.concatenate([ex_hi, ex_hi, ex_lo], 1)
-    g = turn * waves[:, None] * ix(32)[None, :] / 256
-    ey = np.zeros((2, 32, 8, 2, 8, 16))
-    for x in range(8):
-        for blk in range(2):
-            ey[0, :, x, blk, x, :] = np.cos(g[:, blk * 16:blk * 16 + 16])
-            ey[1, :, x, blk, x, :] = -np.sin(g[:, blk * 16:blk * 16 + 16])
-    ey = ey.reshape(2, 16, 2, 8, 256).transpose(0, 2, 1, 3, 4)
-    ey_hi, ey_lo = np_split(ey.reshape(512, 256))
-    h = turn * (waves[None, :] * ix(8)[:, None] % 8) / 8
-    h = np.repeat(h.reshape(8, 16, 2).transpose(0, 2, 1).reshape(8, 32), 8, axis=1)
+    ey = []
+    for apart in (1, 4):
+        points = (apart * 16 * ix(2)[:, None] + ix(16)[None, :]).reshape(32)
+        g = turn * (waves[:, None] * points[None, :] % 256) / 256
+        t = np.zeros((2, 32, 8, 2, 8, 16))
+        for x in range(8):
+            for blk in range(2):
+                t[0, :, x, blk, x, :] = np.cos(g[:, blk * 16:blk * 16 + 16])
+                t[1, :, x, blk, x, :] = -np.sin(g[:, blk * 16:blk * 16 + 16])
+        t = t.reshape(2, 16, 2, 8, 256).transpose(0, 2, 1, 3, 4)
+        ey.extend(np_split(t.reshape(512, 256)))
+    h = turn * (waves[None, :] * ix(16)[:, None] % 16) / 16
+    h = np.repeat(h.reshape(16, 16, 2).transpose(0, 2, 1).reshape(16, 32), 8, axis=1)
     tw_i = np.stack([np.cos(h), np.sin(h)], 0).astype(np.float32)
     ez = np.zeros((16, 2, 2, 2, 2, 256))
     weight = np.where(ix(32) == 0, 1.0, 2.0)[:, None]
@@ -102,7 +105,7 @@
     inv_z = np.concatenate([ez_hi, ez_hi, ez_lo], 0)
     return dict(
         fwd_z=fwd_z, by=np.stack([by_hi, by_lo], 0), tw_y=tw_y, bx=bx, tw_x=tw_x, sel=sel,
-        inv_x=inv_x, ey=np.stack([ey_hi, ey_lo], 0), tw_i=tw_i, inv_z=inv_z,
+        inv_x=inv_x, ey=np.stack(ey, 0), tw_i=tw_i, inv_z=inv_z,
     )
 
 
@@ -209,10 +212,15 @@
     return [jnp.concatenate([t[:64], t[64:]], 1) for t in (arrived.T, other.T)]
 
 
-def inverse_y(plain, other, tw_c, tw_s, ey_hi, ey_lo):
+def swapped(plain):
+    even = lax.broadcasted_iota(jnp.int32, plain.shape, 0) % 2 == 0
+    rows = plain.shape[0]
+    return jnp.where(even, pltpu.roll(plain, rows - 1, 0), -pltpu.roll(plain, 1, 0))
+
+
+def inverse_y(plain, other, phases, ey_hi, ey_lo):
     his, los = [], []
-    for m in range(8):
-        tc, ts = tw_c[m:m + 1, :], tw_s[m:m + 1, :]
+    for tc, ts in phases:
         hi, lo = split(jnp.concatenate([plain * tc - other * ts, other * tc + plain * ts], 1))
         his.append(hi)
         los.append(lo)
@@ -240,7 +248,7 @@
 COL_STEPS = sorted(
     ((a, b) for a in range(4) for b in range(4) if a or b),
     key=lambda s: (-ring(s[0], 4) - ring(s[1], 4), s))
-PIECES = ((0, 8), (8, 8), (16, 8), (24, 8))
+PIECES = ((16, 8), (24, 8))
 
 
 def layer_kernel(*refs):
@@ -249,10 +257,12 @@
     here, refs = refs[:18], refs[18:]
     (step_ref, v_ref, t_ref, fz_ref, by_ref, twy_ref, bx_ref, twx_ref, lift_ref, bias_ref, lw_ref,
      lb_ref, w_ref, sel_ref, ix_ref, ey_ref, twi_ref, iz_ref) = here
-    (adv_ref, local_ref, s1, r1, s2, r2, s3, r3, s4, g_ref, rows_ref,
-     load_sem, send1, recv1, send2, recv2, send3, recv3, send4, recv4) = refs
+    (adv_ref, local_ref, s1, r1, s2, r2, s3, r3, s4, met, s5, g_ref, rows_ref,
+     load_sem, send1, recv1, send2, recv2, send3, recv3, send4, recv4, send_m, recv_m, send5,
+     recv5) = refs
     r = lax.axis_index("row")
     c = lax.axis_index("col")
+    cy, cx = c // 4, c % 4
     row_peers = [((r // 2 + a) % 8) * 2 + (r + b) % 2 for a, b in ROW_STEPS]
     col_peers = [((c // 4 + a) % 4) * 4 + (c + b) % 4 for a, b in COL_STEPS]
 
@@ -343,34 +353,74 @@
         ])
         r3[half, r] = s3[half, r]
 
+    def arrived_half(half):
+        for copy in third[half]:
+            copy.wait_recv()
+        return turned(r3[half].reshape(128, 128), pltpu.roll)
+
+    def phase(k):
+        return twi_ref[0, pl.ds(k, 1), :], twi_ref[1, pl.ds(k, 1), :]
+
+    plain, _ = arrived_half(0)
+    met[0, cx] = plain[:32]
+    met[1, cy] = plain[32:]
+    meet = []
+    for d in (2, 1, 3):
+        meet.append(to_col(met.at[0, cx], met.at[0, cx], send_m.at[0, d], recv_m.at[0, d],
+                           4 * cy + (cx + d) % 4))
+        meet.append(to_col(met.at[1, cy], met.at[1, cy], send_m.at[1, d], recv_m.at[1, d],
+                           4 * ((cy + d) % 4) + cx))
+
+    plain, other = arrived_half(1)
     fourth = []
     for piece, (start, count) in enumerate(PIECES):
-        if start % 16 == 0:
-            half = start // 16
-            for copy in third[half]:
-                copy.wait_recv()
-            plain, other = turned(r3[half].reshape(128, 128), pltpu.roll)
         rows = 4 * count
-        first_row = 4 * (start % 16)
-        h = inverse_y(
-            plain[first_row:first_row + rows], other[first_row:first_row + rows],
-            twi_ref[0], twi_ref[1], ey_ref[0], ey_ref[1])
-        span = pl.ds(4 * start, rows)
+        near = slice(4 * (start - 16), 4 * (start - 16) + rows)
+        h = inverse_y(plain[near], other[near], [phase(2 * m) for m in range(8)],
+                      ey_ref[0], ey_ref[1])
         for dest in range(N):
             m, b = dest // 2, dest % 2
-            s4[dest, span, :] = h[rows * m:rows * m + rows, 128 * b:128 * b + 128]
+            s4[dest, near, :] = h[rows * m:rows * m + rows, 128 * b:128 * b + 128]
+        span = pl.ds(4 * start, rows)
         fourth.append([
-            to_col(s4.at[peer, span], g_ref.at[c, span], send4.at[piece, k], recv4.at[piece, k],
-                   peer)
+            to_col(s4.at[peer, pl.ds(near.start, rows)], g_ref.at[cy, cx, span],
+                   send4.at[piece, k], recv4.at[piece, k], peer)
             for k, peer in enumerate(col_peers)
         ])
-        g_ref[c, span, :] = s4[c, span, :]
-
-    for piece, (start, count) in enumerate(PIECES):
-        for copy in fourth[piece]:
-            copy.wait_recv()
+        g_ref[cy, cx, span, :] = s4[c, near, :]
+
+    for copy in meet:
+        copy.wait_recv()
+    fifth = []
+    for sub in range(2):
+        fifth.append([])
+        for axis in range(2):
+            plain = met[axis, :, 16 * sub:16 * sub + 16, :].reshape(64, 256)
+            phases = [phase(8 * m + cx) if axis == 0 else phase(4 * cy + 2 * m) for m in range(2)]
+            table = 2 if axis == 0 else 0
+            h = inverse_y(plain, swapped(plain), phases, ey_ref[table], ey_ref[table + 1])
+            for t in range(4):
+                m, b = t // 2, t % 2
+                s5[axis, sub, t] = h[64 * m:64 * m + 64, 128 * b:128 * b + 128].reshape(4, 16, 128)
+            span = pl.ds(32 * axis + 16 * sub, 16)
+            for d in (2, 1, 3):
+                sems = send5.at[axis, sub, d], recv5.at[axis, sub, d]
+                if axis == 0:
+                    t = (cy + d) % 4
+                    fifth[sub].append(
+                        to_col(s5.at[0, sub, t], g_ref.at[cy, :, span], *sems, 4 * t + cx))
+                else:
+                    t = (cx + d) % 4
+                    fifth[sub].append(
+                        to_col(s5.at[1, sub, t], g_ref.at[:, cx, span], *sems, 4 * cy + t))
+            if axis == 0:
+                g_ref[cy, :, span, :] = s5[0, sub, cy]
+            else:
+                g_ref[:, cx, span, :] = s5[1, sub, cx]
+
+    def cells(start, count):
         for o in range(start, start + count, 2):
-            values = inverse_z(g_ref[:, 4 * o:4 * o + 8, :].reshape(128, 128), iz_ref[...])
+            values = inverse_z(g_ref[:, :, 4 * o:4 * o + 8, :].reshape(128, 128), iz_ref[...])
             for k in range(2):
                 scale = [
                     jnp.concatenate([local_ref[o + k:o + k + 1, 128 * j:128 * j + 128]] * 2, 1)
@@ -382,7 +432,17 @@
                     for j in range(3):
                         value += scale[j] * adv_ref[j, cell, :]
                     out_ref[o + k, x] = activate(value).astype(BF16)
-    for copies in [first, second] + third + fourth:
+
+    for piece, (start, count) in enumerate(PIECES):
+        for copy in fourth[piece]:
+            copy.wait_recv()
+        cells(start, count)
+    for sub in range(2):
+        for copy in fifth[sub]:
+            copy.wait_recv()
+        cells(4 * sub, 4)
+        cells(8 + 4 * sub, 4)
+    for copies in [first, second, meet] + third + fourth + fifth:
         for copy in copies:
             copy.wait_send()
 
@@ -408,10 +468,12 @@
             pltpu.VMEM((256, 128), F32), pltpu.VMEM((16, 16, 128), F32),
             pltpu.VMEM((16, 8, 128), F32), pltpu.VMEM((16, 8, 128), F32),
             pltpu.VMEM((2, 16, 8, 128), F32), pltpu.VMEM((2, 16, 8, 128), F32),
-            pltpu.VMEM((16, 128, 128), F32), pltpu.VMEM((16, 128, 128), F32),
+            pltpu.VMEM((16, 64, 128), F32), pltpu.VMEM((2, 4, 32, 256), F32),
+            pltpu.VMEM((2, 2, 4, 4, 16, 128), F32), pltpu.VMEM((4, 4, 128, 128), F32),
             pltpu.VMEM((8, 32), F32),
             dma((len(far),)), dma((N,)), dma((N,)), dma((N,)), dma((N,)),
             dma((2, N)), dma((2, N)), dma((len(PIECES), N)), dma((len(PIECES), N)),
+            dma((2, 4)), dma((2, 4)), dma((2, 2, 4)), dma((2, 2, 4)),
         ],
         compiler_params=pltpu.CompilerParams(
             collective_id=0, has_side_effects=True, vmem_limit_bytes=VMEM_LIMIT),

time: 47 us -> 44.8 us (0.953)
  Pallas kernels: 45 us -> 42.7 us
    pallas_call x1, Pallas kernels: 45 us -> 42.7 us  [per_device(): pl.pallas_call(layer_kernel, out_shape=pltpu.VMEM((32, 8, 16, 256), BF16)...]
where the time goes in v4:
time: 44.8 us; the launch traced here: 44.7 us
  Pallas kernels  42.7 us (95%)
  local copies, waits for them, and re-layouts  1.32 us (3%)
  between operations  0.66 us (1%)
    pallas_call x1, Pallas kernels, per_device(): pl.pallas_call(layer_kernel, out_shape=pltpu.VMEM((32, 8, 16, 256), BF16)...  42.7 us
    unnamed x1, local copies, waits for them, and re-layouts  1.32 us

profile of v4, /device:TPU:1, one launch (start us, length us, event | category | flops | bytes accessed | tf_op | source)
XLA Modules:
  0.0 44.7 jit_solution(10488199065970161889)
XLA Ops:
  0.7 42.7 %layer.1 = bf16[32,8,16,256]{3,2,1,0:T(8,128)(2,1)S(1)} custom-call(f32[1]{0:T(128)S(6)} %copy.21.refs_0_, f32[3,128,256]{2,1,0:T(8,128)} %bitcast.7, f32[3,128,256]{2,1,0:T(8,128)} %bitcast.8, bf16[64,768]{1,0:T(8,128)(2,1)} %constant.20.clone.refs_3_, bf16[2,256,512]{2,1,0:T(8,128)(2,1)} %constant.21.clone.refs_4_, f32[2,16,256]{2,1,0:T(8,128)} %constant.22.clone.refs_5_, ...), custom_call_target="tpu_custom_call" | custom-call | tf_op jit(solution)/shard_map/layer/pallas_call | solution.py:461
  43.4 1.3 %copy.20 = bf16[1,32,8,16,256]{4,3,2,1,0:T(8,128)(2,1)} copy(bf16[1,32,8,16,256]{4,3,2,1,0:T(8,128)(2,1)S(1)} %bitcast.6) | data formatting | bytes 4194304

commit v5 on v4

--- a/solution.py
+++ b/solution.py
@@ -248,7 +248,8 @@
 COL_STEPS = sorted(
     ((a, b) for a in range(4) for b in range(4) if a or b),
     key=lambda s: (-ring(s[0], 4) - ring(s[1], 4), s))
-PIECES = ((16, 8), (24, 8))
+PIECES = ((16, 8),)
+MEETS = ((0, 8, 8, (4, 4)), (24, 28, 4, (2, 2)))
 
 
 def layer_kernel(*refs):
@@ -361,17 +362,23 @@
     def phase(k):
         return twi_ref[0, pl.ds(k, 1), :], twi_ref[1, pl.ds(k, 1), :]
 
+    def meet(entry, plain):
+        copies = []
+        for axis in range(2):
+            start, count = MEETS[entry][axis], MEETS[entry][2]
+            first_row = 4 * (start % 16)
+            place = met.at[axis, cx if axis == 0 else cy, pl.ds(32 * entry, 4 * count)]
+            place[...] = plain[first_row:first_row + 4 * count]
+            for d in (2, 1, 3):
+                peer = 4 * cy + (cx + d) % 4 if axis == 0 else 4 * ((cy + d) % 4) + cx
+                copies.append(to_col(
+                    place, place, send_m.at[entry, axis, d], recv_m.at[entry, axis, d], peer))
+        return copies
+
     plain, _ = arrived_half(0)
-    met[0, cx] = plain[:32]
-    met[1, cy] = plain[32:]
-    meet = []
-    for d in (2, 1, 3):
-        meet.append(to_col(met.at[0, cx], met.at[0, cx], send_m.at[0, d], recv_m.at[0, d],
-                           4 * cy + (cx + d) % 4))
-        meet.append(to_col(met.at[1, cy], met.at[1, cy], send_m.at[1, d], recv_m.at[1, d],
-                           4 * ((cy + d) % 4) + cx))
-
+    meets = [meet(0, plain)]
     plain, other = arrived_half(1)
+    meets.append(meet(1, plain))
     fourth = []
     for piece, (start, count) in enumerate(PIECES):
         rows = 4 * count
@@ -389,34 +396,44 @@
         ])
         g_ref[cy, cx, span, :] = s4[c, near, :]
 
-    for copy in meet:
-        copy.wait_recv()
     fifth = []
-    for sub in range(2):
-        fifth.append([])
-        for axis in range(2):
-            plain = met[axis, :, 16 * sub:16 * sub + 16, :].reshape(64, 256)
-            phases = [phase(8 * m + cx) if axis == 0 else phase(4 * cy + 2 * m) for m in range(2)]
-            table = 2 if axis == 0 else 0
-            h = inverse_y(plain, swapped(plain), phases, ey_ref[table], ey_ref[table + 1])
-            for t in range(4):
-                m, b = t // 2, t % 2
-                s5[axis, sub, t] = h[64 * m:64 * m + 64, 128 * b:128 * b + 128].reshape(4, 16, 128)
-            span = pl.ds(32 * axis + 16 * sub, 16)
-            for d in (2, 1, 3):
-                sems = send5.at[axis, sub, d], recv5.at[axis, sub, d]
+    for entry, (start_x, start_y, _, parts) in enumerate(MEETS):
+        for copy in meets[entry]:
+            copy.wait_recv()
+        done = 0
+        for count in parts:
+            part = len(fifth)
+            rows = 4 * count
+            copies = []
+            for axis, start in enumerate((start_x, start_y)):
+                far = pl.ds(32 * entry + 4 * done, rows)
+                plain = met[axis, :, far, :].reshape(4 * rows, 256)
+                phases = [
+                    phase(8 * m + cx) if axis == 0 else phase(4 * cy + 2 * m) for m in range(2)]
+                table = 2 if axis == 0 else 0
+                h = inverse_y(plain, swapped(plain), phases, ey_ref[table], ey_ref[table + 1])
+                for t in range(4):
+                    m, b = t // 2, t % 2
+                    s5[part, axis, t, :, :rows] = h[
+                        4 * rows * m:4 * rows * m + 4 * rows, 128 * b:128 * b + 128
+                    ].reshape(4, rows, 128)
+                span = pl.ds(4 * (start + done), rows)
+                for d in (2, 1, 3):
+                    sems = send5.at[part, axis, d], recv5.at[part, axis, d]
+                    if axis == 0:
+                        t = (cy + d) % 4
+                        copies.append(
+                            to_col(s5.at[part, 0, t, :, pl.ds(0, rows)], g_ref.at[cy, :, span], *sems, 4 * t + cx))
+                    else:
+                        t = (cx + d) % 4
+                        copies.append(
+                            to_col(s5.at[part, 1, t, :, pl.ds(0, rows)], g_ref.at[:, cx, span], *sems, 4 * cy + t))
                 if axis == 0:
-                    t = (cy + d) % 4
-                    fifth[sub].append(
-                        to_col(s5.at[0, sub, t], g_ref.at[cy, :, span], *sems, 4 * t + cx))
+                    g_ref[cy, :, span, :] = s5[part, 0, cy, :, :rows]
                 else:
-                    t = (cx + d) % 4
-                    fifth[sub].append(
-                        to_col(s5.at[1, sub, t], g_ref.at[:, cx, span], *sems, 4 * cy + t))
-            if axis == 0:
-                g_ref[cy, :, span, :] = s5[0, sub, cy]
-            else:
-                g_ref[:, cx, span, :] = s5[1, sub, cx]
+                    g_ref[:, cx, span, :] = s5[part, 1, cx, :, :rows]
+            fifth.append((copies, start_x + done, start_y + done, count))
+            done += count
 
     def cells(start, count):
         for o in range(start, start + count, 2):
@@ -437,12 +454,12 @@
         for copy in fourth[piece]:
             copy.wait_recv()
         cells(start, count)
-    for sub in range(2):
-        for copy in fifth[sub]:
+    for copies, start_x, start_y, count in fifth:
+        for copy in copies:
             copy.wait_recv()
-        cells(4 * sub, 4)
-        cells(8 + 4 * sub, 4)
-    for copies in [first, second, meet] + third + fourth + fifth:
+        cells(start_x, count)
+        cells(start_y, count)
+    for copies in [first, second] + third + meets + fourth + [entry[0] for entry in fifth]:
         for copy in copies:
             copy.wait_send()
 
@@ -468,12 +485,12 @@
             pltpu.VMEM((256, 128), F32), pltpu.VMEM((16, 16, 128), F32),
             pltpu.VMEM((16, 8, 128), F32), pltpu.VMEM((16, 8, 128), F32),
             pltpu.VMEM((2, 16, 8, 128), F32), pltpu.VMEM((2, 16, 8, 128), F32),
-            pltpu.VMEM((16, 64, 128), F32), pltpu.VMEM((2, 4, 32, 256), F32),
-            pltpu.VMEM((2, 2, 4, 4, 16, 128), F32), pltpu.VMEM((4, 4, 128, 128), F32),
+            pltpu.VMEM((16, 64, 128), F32), pltpu.VMEM((2, 4, 64, 256), F32),
+            pltpu.VMEM((4, 2, 4, 4, 16, 128), F32), pltpu.VMEM((4, 4, 128, 128), F32),
             pltpu.VMEM((8, 32), F32),
             dma((len(far),)), dma((N,)), dma((N,)), dma((N,)), dma((N,)),
             dma((2, N)), dma((2, N)), dma((len(PIECES), N)), dma((len(PIECES), N)),
-            dma((2, 4)), dma((2, 4)), dma((2, 2, 4)), dma((2, 2, 4)),
+            dma((2, 2, 4)), dma((2, 2, 4)), dma((4, 2, 4)), dma((4, 2, 4)),
         ],
         compiler_params=pltpu.CompilerParams(
             collective_id=0, has_side_effects=True, vmem_limit_bytes=VMEM_LIMIT),

time: 44.8 us -> 43.5 us (0.971)
  Pallas kernels: 42.7 us -> 41.4 us
    pallas_call x1, Pallas kernels: 42.7 us -> 41.4 us  [per_device(): pl.pallas_call(layer_kernel, out_shape=pltpu.VMEM((32, 8, 16, 256), BF16)...]
where the time goes in v5:
time: 43.5 us; the launch traced here: 43.4 us
  Pallas kernels  41.4 us (95%)
  local copies, waits for them, and re-layouts  1.32 us (3%)
  between operations  0.66 us (2%)
    pallas_call x1, Pallas kernels, per_device(): pl.pallas_call(layer_kernel, out_shape=pltpu.VMEM((32, 8, 16, 256), BF16)...  41.4 us
    unnamed x1, local copies, waits for them, and re-layouts  1.32 us

profile of v5, /device:TPU:1, one launch (start us, length us, event | category | flops | bytes accessed | tf_op | source)
XLA Modules:
  0.0 43.4 jit_solution(18018274403944629350)
XLA Ops:
  0.7 41.4 %layer.1 = bf16[32,8,16,256]{3,2,1,0:T(8,128)(2,1)S(1)} custom-call(f32[1]{0:T(128)S(6)} %copy.21.refs_0_, f32[3,128,256]{2,1,0:T(8,128)} %bitcast.7, f32[3,128,256]{2,1,0:T(8,128)} %bitcast.8, bf16[64,768]{1,0:T(8,128)(2,1)} %constant.20.clone.refs_3_, bf16[2,256,512]{2,1,0:T(8,128)(2,1)} %constant.21.clone.refs_4_, f32[2,16,256]{2,1,0:T(8,128)} %constant.22.clone.refs_5_, ...), custom_call_target="tpu_custom_call" | custom-call | tf_op jit(solution)/shard_map/layer/pallas_call | solution.py:478
  42.1 1.3 %copy.20 = bf16[1,32,8,16,256]{4,3,2,1,0:T(8,128)(2,1)} copy(bf16[1,32,8,16,256]{4,3,2,1,0:T(8,128)(2,1)S(1)} %bitcast.6) | data formatting | bytes 4194304

commit v6 on v5

--- a/solution.py
+++ b/solution.py
@@ -76,7 +76,6 @@
     d = turn * (waves[None, :] * ix(16)[:, None] % 16) / 16
     d = np.tile(d, (1, 16))
     tw_x = np.stack([np.cos(d), np.sin(d)], 0).astype(np.float32)
-    sel = (ix(512)[:, None] // 32 == ix(128)[None, :] // 4 % 16).astype(jnp.bfloat16)
     f = turn * (waves[None, :] * ix(128)[:, None] % 128) / 128
     ex_hi, ex_lo = np_split(np.concatenate([np.cos(f), np.sin(f)], 1))
     inv_x = np.concatenate([ex_hi, ex_hi, ex_lo], 1)
@@ -104,7 +103,7 @@
     ez_hi, ez_lo = np_split(ez.reshape(128, 512))
     inv_z = np.concatenate([ez_hi, ez_hi, ez_lo], 0)
     return dict(
-        fwd_z=fwd_z, by=np.stack([by_hi, by_lo], 0), tw_y=tw_y, bx=bx, tw_x=tw_x, sel=sel,
+        fwd_z=fwd_z, by=np.stack([by_hi, by_lo], 0), tw_y=tw_y, bx=bx, tw_x=tw_x,
         inv_x=inv_x, ey=np.stack(ey, 0), tw_i=tw_i, inv_z=inv_z,
     )
 
@@ -143,65 +142,77 @@
     return u[:32] + u[32:] + dot(hi, bx_lo)
 
 
-def lift_table(rows):
-    i = lax.broadcasted_iota(jnp.int32, (32, 128), 0)
-    lane = lax.broadcasted_iota(jnp.int32, (32, 128), 1)
-    wide = dot_exact(rows, jnp.where(lane % 32 == i, 1.0, 0.0).astype(F32))
-    upper = lax.broadcasted_iota(jnp.int32, (8, 128), 0) < 4
-    return jnp.concatenate([jnp.where(upper, wide, 0.0), jnp.where(upper, 0.0, wide)], 1)
+def dot_nt_exact(a, b):
+    return lax.dot_general(
+        a, b, (((1,), (1,)), ((), ())), precision=lax.Precision.HIGHEST, preferred_element_type=F32)
+
+
+def spread(rows):
+    return jnp.concatenate([jnp.broadcast_to(rows[j:j + 1], (128, 32)) for j in range(4)], 0)
+
+
+def identity():
+    return jnp.where(
+        lax.broadcasted_iota(jnp.int32, (32, 32), 0) == lax.broadcasted_iota(
+            jnp.int32, (32, 32), 1), 1.0, 0.0).astype(F32)
 
 
 def local_table(rows, local_weight, local_bias):
-    wide = jnp.concatenate([jnp.broadcast_to(rows[j:j + 1], (128, 32)) for j in range(4)], 0)
-    scale = lax.dot_general(
-        local_weight, wide, (((1,), (1,)), ((), ())), precision=lax.Precision.HIGHEST,
-        preferred_element_type=F32)
-    same = lax.broadcasted_iota(jnp.int32, (32, 32), 0) == lax.broadcasted_iota(
-        jnp.int32, (32, 32), 1)
-    bias = lax.dot_general(
-        jnp.where(same, 1.0, 0.0).astype(F32), jnp.broadcast_to(local_bias, (128, 32)),
-        (((1,), (1,)), ((), ())), precision=lax.Precision.HIGHEST, preferred_element_type=F32)
+    scale = dot_nt_exact(local_weight, spread(rows))
+    bias = dot_nt_exact(identity(), jnp.broadcast_to(local_bias, (128, 32)))
     return jnp.concatenate([scale[:, :384], scale[:, 384:] + bias], 1)
 
 
-def lifted_coeffs(total, first, lift):
-    row = lax.broadcasted_iota(jnp.int32, (8, 128), 0)
-    lane = lax.broadcasted_iota(jnp.int32, (8, 128), 1)
-    total = total * (1.0 / 8388608.0) + jnp.where((row == 3) & (lane == 0), first, 0.0)
-    return dot_exact(total.T, lift)
-
-
-def mix(coeffs, weight, sel):
-    his, los = [], []
-    for ky in range(2):
-        for kz in range(2):
-            cr = coeffs[64 * ky:64 * ky + 32, 128 * kz:128 * kz + 128]
-            ci = coeffs[64 * ky + 32:64 * ky + 64, 128 * kz:128 * kz + 128]
-            cr4 = jnp.concatenate([cr] * 4, 1)
-            ci4 = jnp.concatenate([ci] * 4, 1)
-            wr = weight(0, ky, kz).astype(F32)
-            wi = weight(1, ky, kz).astype(F32)
-            for value in (wr * cr4 - wi * ci4, wr * ci4 + wi * cr4):
-                hi, lo = split(value)
-                his.append(hi)
-                los.append(lo)
-    return dot(jnp.concatenate(his, 0), sel) + dot(jnp.concatenate(los, 0), sel)
-
-
-def inverse_x(mixed, inv_x):
-    lane = lax.broadcasted_iota(jnp.int32, (32, 128), 1)
-    kind = lane % 4
-    tops, bottoms = [], []
-    for ky in range(2):
-        block = [mixed[128 * ky + 32 * n:128 * ky + 32 * n + 32] for n in range(4)]
-
-        def pick(a, b, c, d):
-            return jnp.where(kind == 0, a, jnp.where(kind == 1, b, jnp.where(kind == 2, c, d)))
-
-        tops.append(pick(block[0], block[1], block[2], block[3]))
-        bottoms.append(pick(-block[1], block[0], -block[3], block[2]))
-    top = jnp.where(lane < 64, tops[0], tops[1])
-    bottom = jnp.where(lane < 64, bottoms[0], bottoms[1])
+def lane(shape):
+    return lax.broadcasted_iota(jnp.int32, shape, len(shape) - 1)
+
+
+def lift_tables(rows):
+    columns = dot_nt_exact(identity(), spread(rows))
+    own = lax.broadcasted_iota(jnp.int32, (512, 128), 0) // 32 == lane((512, 128)) // 4 % 16
+    return [
+        split(jnp.where(own, jnp.concatenate([columns[:, 128 * j:128 * j + 128]] * 16, 0), 0.0))
+        for j in range(4)
+    ]
+
+
+def lifted_weights(blocks, lift):
+    stacked = jnp.concatenate([b for part in blocks for row in part for b in row], 0)
+    u = dot(stacked, lift[0]) + dot(stacked, lift[1])
+    first_kz, first_ky = lane((32, 128)) % 4 < 2, lane((32, 128)) < 64
+    out = []
+    for part in range(2):
+        b = [u[128 * part + 32 * n:128 * part + 32 * n + 32] for n in range(4)]
+        out.append(jnp.where(
+            first_ky, jnp.where(first_kz, b[0], b[1]), jnp.where(first_kz, b[2], b[3])))
+    return out
+
+
+def spread_modes(total, first):
+    row, column = lax.broadcasted_iota(jnp.int32, (8, 128), 0), lane((8, 128))
+    total = total * (1.0 / 8388608.0) + jnp.where((row == 3) & (column == 0), first, 0.0)
+    row, column = lax.broadcasted_iota(jnp.int32, (8, 512), 0), lane((8, 512))
+    place = (row % 4 == column // 128) & (row // 4 == column % 4 // 2)
+    place = jnp.where(place, 1.0, 0.0).astype(BF16)
+    hi, lo = split(total.T)
+    u = dot(hi, place) + dot(lo, place)
+    first_ky = lane((32, 128)) < 64
+    return [
+        [jnp.where(first_ky, u[32 * part:32 * part + 32, 128 * j:128 * j + 128],
+                   u[64 + 32 * part:96 + 32 * part, 128 * j:128 * j + 128]) for part in range(2)]
+        for j in range(4)
+    ]
+
+
+def inverse_x(weights, modes, inv_x):
+    real, imag = 0.0, 0.0
+    for j in range(4):
+        wr, wi = weights(0, j), weights(1, j)
+        mr, mi = modes[j]
+        real += wr * mr - wi * mi
+        imag += wr * mi + wi * mr
+    even = lane((32, 128)) % 2 == 0
+    top, bottom = jnp.where(even, real, imag), jnp.where(even, -imag, real)
     hi, lo = split(jnp.concatenate([top, bottom], 0))
     return dot(inv_x, jnp.concatenate([hi, lo, hi], 0))
 
@@ -253,12 +264,12 @@
 
 
 def layer_kernel(*refs):
-    hbm, refs = refs[:18], refs[18:]
+    hbm, refs = refs[:17], refs[17:]
     out_ref, refs = refs[0], refs[1:]
-    here, refs = refs[:18], refs[18:]
+    here, refs = refs[:17], refs[17:]
     (step_ref, v_ref, t_ref, fz_ref, by_ref, twy_ref, bx_ref, twx_ref, lift_ref, bias_ref, lw_ref,
-     lb_ref, w_ref, sel_ref, ix_ref, ey_ref, twi_ref, iz_ref) = here
-    (adv_ref, local_ref, s1, r1, s2, r2, s3, r3, s4, met, s5, g_ref, rows_ref,
+     lb_ref, w_ref, ix_ref, ey_ref, twi_ref, iz_ref) = here
+    (adv_ref, local_ref, s1, r1, s2, r2, s3, r3, s4, met, s5, g_ref, rows_ref, wl_ref,
      load_sem, send1, recv1, send2, recv2, send3, recv3, send4, recv4, send_m, recv_m, send5,
      recv5) = refs
     r = lax.axis_index("row")
@@ -318,8 +329,13 @@
     for k in (0, 4):
         rows_ref[k:k + 3] = lift_ref[...]
         rows_ref[k + 3:k + 4] = bias_ref[...]
-    lift = lift_table(rows_ref[...])
     local_ref[...] = local_table(rows_ref[...], lw_ref[...], lb_ref[...])
+    lifts = lift_tables(rows_ref[...])
+    for half in range(2):
+        blocks = [[[w_ref[part, ky, kz, :, 512 * half:512 * half + 512] for kz in range(2)]
+                   for ky in range(2)] for part in range(2)]
+        for j in range(4):
+            wl_ref[half, 0, j], wl_ref[half, 1, j] = lifted_weights(blocks, lifts[j])
     for copy in first:
         copy.wait_recv()
 
@@ -340,14 +356,11 @@
     total = jnp.sum(r2[...], axis=0)
 
     origin = jnp.where((r == 0) & (c == 0), 1.0, 0.0).astype(F32)
-    coeffs = lifted_coeffs(total, origin, lift)
+    modes = spread_modes(total, origin)
     third = []
     for half in range(2):
-        mixed = mix(
-            coeffs,
-            lambda part, ky, kz: w_ref[part, ky, kz, :, 512 * half:512 * half + 512],
-            sel_ref[...])
-        s3[half] = inverse_x(mixed, ix_ref[...]).reshape(16, 8, 128)
+        s3[half] = inverse_x(
+            lambda part, j: wl_ref[half, part, j], modes, ix_ref[...]).reshape(16, 8, 128)
         third.append([
             to_row(s3.at[half, peer], r3.at[half, r], send3.at[half, k], recv3.at[half, k], peer)
             for k, peer in enumerate(row_peers)
@@ -471,7 +484,7 @@
     far = [
         step_size, velocity.reshape(3, 128, 256), tendency.reshape(3, 128, 256), const["fwd_z"],
         const["by"], const["tw_y"], const["bx"], const["tw_x"], lift_weight.T, lift_bias[None, :],
-        local_weight, local_bias[None, :], spectral_weight, const["sel"], const["inv_x"],
+        local_weight, local_bias[None, :], spectral_weight, const["inv_x"],
         const["ey"], const["tw_i"], const["inv_z"],
     ]
     dma = pltpu.SemaphoreType.DMA
@@ -487,7 +500,7 @@
             pltpu.VMEM((2, 16, 8, 128), F32), pltpu.VMEM((2, 16, 8, 128), F32),
             pltpu.VMEM((16, 64, 128), F32), pltpu.VMEM((2, 4, 64, 256), F32),
             pltpu.VMEM((4, 2, 4, 4, 16, 128), F32), pltpu.VMEM((4, 4, 128, 128), F32),
-            pltpu.VMEM((8, 32), F32),
+            pltpu.VMEM((8, 32), F32), pltpu.VMEM((2, 2, 4, 32, 128), F32),
             dma((len(far),)), dma((N,)), dma((N,)), dma((N,)), dma((N,)),
             dma((2, N)), dma((2, N)), dma((len(PIECES), N)), dma((len(PIECES), N)),
             dma((2, 2, 4)), dma((2, 2, 4)), dma((4, 2, 4)), dma((4, 2, 4)),

time: 43.5 us -> 43.2 us (level)
  no operation moved by 1% of the time
where the time goes in v6:
time: 43.2 us; the launch traced here: 43.1 us
  Pallas kernels  41.1 us (95%)
  local copies, waits for them, and re-layouts  1.32 us (3%)
  between operations  0.66 us (2%)
    pallas_call x1, Pallas kernels, per_device(): pl.pallas_call(layer_kernel, out_shape=pltpu.VMEM((32, 8, 16, 256), BF16)...  41.1 us
    unnamed x1, local copies, waits for them, and re-layouts  1.32 us

profile of v6, /device:TPU:1, one launch (start us, length us, event | category | flops | bytes accessed | tf_op | source)
XLA Modules:
  0.0 43.1 jit_solution(1151487684883272202)
XLA Ops:
  0.7 41.1 %layer.1 = bf16[32,8,16,256]{3,2,1,0:T(8,128)(2,1)S(1)} custom-call(f32[1]{0:T(128)S(6)} %copy.20.refs_0_, f32[3,128,256]{2,1,0:T(8,128)} %bitcast.7, f32[3,128,256]{2,1,0:T(8,128)} %bitcast.8, bf16[64,768]{1,0:T(8,128)(2,1)} %constant.18.clone.refs_3_, bf16[2,256,512]{2,1,0:T(8,128)(2,1)} %constant.19.clone.refs_4_, f32[2,16,256]{2,1,0:T(8,128)} %constant.20.clone.refs_5_, ...), custom_call_target="tpu_custom_call" | custom-call | tf_op jit(solution)/shard_map/layer/pallas_call | solution.py:491
  41.8 1.3 %copy.19 = bf16[1,32,8,16,256]{4,3,2,1,0:T(8,128)(2,1)} copy(bf16[1,32,8,16,256]{4,3,2,1,0:T(8,128)(2,1)S(1)} %bitcast.6) | data formatting | bytes 4194304

commit v7 on v6

--- a/solution.py
+++ b/solution.py
@@ -50,7 +50,7 @@
     z_angle = turn * (ix(32)[:, None] * ix(256)[None, :] % 256) / 256
     z_hi, z_lo = np_split(np.concatenate([np.cos(z_angle), -np.sin(z_angle)], 0))
     fwd_z = np.concatenate([z_hi, z_lo, z_hi], 1)
-    fwd_z = fwd_z.reshape(2, 16, 2, 768).transpose(1, 0, 2, 3).reshape(64, 768)
+    fwd_z = fwd_z.reshape(2, 16, 2, 768).transpose(2, 1, 0, 3).reshape(64, 768)
     a = turn * waves[None, :] * ix(16)[:, None] / 256
     by = np.zeros((2, 8, 16, 2, 32, 8))
     for x in range(8):
@@ -190,9 +190,11 @@
 
 def spread_modes(total, first):
     row, column = lax.broadcasted_iota(jnp.int32, (8, 128), 0), lane((8, 128))
-    total = total * (1.0 / 8388608.0) + jnp.where((row == 3) & (column == 0), first, 0.0)
+    total = jnp.where(row < 6, total * (1.0 / 8388608.0), 0.0)
+    total = total + jnp.where((row == 6) & (column == 0), first, 0.0)
     row, column = lax.broadcasted_iota(jnp.int32, (8, 512), 0), lane((8, 512))
-    place = (row % 4 == column // 128) & (row // 4 == column % 4 // 2)
+    j, kz = column // 128, column % 4 // 2
+    place = ((row < 6) & (row == 3 * kz + j) & (j < 3)) | ((row == 6) & (j == 3) & (kz == 0))
     place = jnp.where(place, 1.0, 0.0).astype(BF16)
     hi, lo = split(total.T)
     u = dot(hi, place) + dot(lo, place)
@@ -312,16 +314,17 @@
     advanced = v_ref[...] + step_ref[0] * t_ref[...]
     adv_ref[...] = advanced
     z = forward_z(advanced.reshape(384, 256), fz_ref[...])
-    s1[pl.ds(3, 64, stride=4), :] = jnp.zeros((64, 128), F32)
-    for j in range(3):
-        s1[pl.ds(j, 64, stride=4), :] = z[:, 128 * j:128 * j + 128]
+    for kz in range(2):
+        for j in range(3):
+            s1[pl.ds(3 * kz + j, 32, stride=8), :] = z[32 * kz:32 * kz + 32, 128 * j:128 * j + 128]
     pl.semaphore_wait(barrier, 2 * (N - 1))
+    used = pl.ds(0, 6)
     first = [
-        to_col(s1.at[pl.ds(pl.multiple_of(16 * peer, 16), 16)], r1.at[c], send1.at[k], recv1.at[k],
-               peer)
+        to_col(s1.reshape(16, 2, 8, 128).at[peer, :, used], r1.at[c, :, used], send1.at[k],
+               recv1.at[k], peer)
         for k, peer in enumerate(col_peers)
     ]
-    r1[c] = s1[pl.ds(pl.multiple_of(16 * c, 16), 16), :]
+    r1[c] = s1[pl.ds(pl.multiple_of(16 * c, 16), 16), :].reshape(2, 8, 128)
     for load in loads[4:]:
         load.wait()
     bx_hi, bx_lo = x_table(
@@ -340,14 +343,14 @@
         copy.wait_recv()
 
     arrived = jnp.concatenate(
-        [r1[:, 8 * part:8 * part + 8, :].reshape(128, 128) for part in range(2)], 1)
+        [r1[:, part].reshape(128, 128) for part in range(2)], 1)
     real, imag = forward_y(arrived, by_ref[0], by_ref[1], twy_ref[0], twy_ref[1])
     partial = forward_x(real, imag, bx_hi, bx_lo, pltpu.roll)
     for g in range(4):
         for k in range(4):
             s2[4 * g + k] = partial[8 * g:8 * g + 8, 128 * k:128 * k + 128]
     second = [
-        to_row(s2.at[peer], r2.at[r], send2.at[k], recv2.at[k], peer)
+        to_row(s2.at[peer, used], r2.at[r, used], send2.at[k], recv2.at[k], peer)
         for k, peer in enumerate(row_peers)
     ]
     r2[r] = s2[r]
@@ -467,14 +470,19 @@
         for copy in fourth[piece]:
             copy.wait_recv()
         cells(start, count)
-    for copies, start_x, start_y, count in fifth:
+    for copies in [first, second] + third + meets + fourth:
+        for copy in copies:
+            copy.wait_send()
+    for part, (copies, start_x, start_y, count) in enumerate(fifth):
+        if part:
+            for copy in fifth[part - 1][0]:
+                copy.wait_send()
         for copy in copies:
             copy.wait_recv()
         cells(start_x, count)
         cells(start_y, count)
-    for copies in [first, second] + third + meets + fourth + [entry[0] for entry in fifth]:
-        for copy in copies:
-            copy.wait_send()
+    for copy in fifth[-1][0]:
+        copy.wait_send()
 
 
 def per_device(
@@ -495,7 +503,7 @@
         out_specs=pl.BlockSpec(memory_space=pltpu.VMEM),
         scratch_shapes=[pltpu.SMEM((1,), F32)] + [pltpu.VMEM(a.shape, a.dtype) for a in far[1:]] + [
             pltpu.VMEM((3, 128, 256), F32), pltpu.VMEM((32, 512), F32),
-            pltpu.VMEM((256, 128), F32), pltpu.VMEM((16, 16, 128), F32),
+            pltpu.VMEM((256, 128), F32), pltpu.VMEM((16, 2, 8, 128), F32),
             pltpu.VMEM((16, 8, 128), F32), pltpu.VMEM((16, 8, 128), F32),
             pltpu.VMEM((2, 16, 8, 128), F32), pltpu.VMEM((2, 16, 8, 128), F32),
             pltpu.VMEM((16, 64, 128), F32), pltpu.VMEM((2, 4, 64, 256), F32),

time: 43.2 us -> 43.1 us (level)
  no operation moved by 1% of the time
where the time goes in v7:
time: 43.1 us; the launch traced here: 43 us
  Pallas kernels  41 us (95%)
  local copies, waits for them, and re-layouts  1.32 us (3%)
  between operations  0.66 us (2%)
    pallas_call x1, Pallas kernels, per_device(): pl.pallas_call(layer_kernel, out_shape=pltpu.VMEM((32, 8, 16, 256), BF16)...  41 us
    unnamed x1, local copies, waits for them, and re-layouts  1.32 us

profile of v7, /device:TPU:1, one launch (start us, length us, event | category | flops | bytes accessed | tf_op | source)
XLA Modules:
  0.0 43.0 jit_solution(6293672593974195548)
XLA Ops:
  0.7 41.0 %layer.1 = bf16[32,8,16,256]{3,2,1,0:T(8,128)(2,1)S(1)} custom-call(f32[1]{0:T(128)S(6)} %copy.20.refs_0_, f32[3,128,256]{2,1,0:T(8,128)} %bitcast.7, f32[3,128,256]{2,1,0:T(8,128)} %bitcast.8, bf16[64,768]{1,0:T(8,128)(2,1)} %constant.18.clone.refs_3_, bf16[2,256,512]{2,1,0:T(8,128)(2,1)} %constant.19.clone.refs_4_, f32[2,16,256]{2,1,0:T(8,128)} %constant.20.clone.refs_5_, ...), custom_call_target="tpu_custom_call" | custom-call | tf_op jit(solution)/shard_map/layer/pallas_call | solution.py:499
  41.7 1.3 %copy.19 = bf16[1,32,8,16,256]{4,3,2,1,0:T(8,128)(2,1)} copy(bf16[1,32,8,16,256]{4,3,2,1,0:T(8,128)(2,1)S(1)} %bitcast.6) | data formatting | bytes 4194304

commit v8 on v6

--- a/solution.py
+++ b/solution.py
@@ -100,7 +100,7 @@
     for o in range(2):
         ez[:, o, :, 0, o, :] = cz
         ez[:, o, :, 1, o, :] = sz
-    ez_hi, ez_lo = np_split(ez.reshape(128, 512))
+    ez_hi, ez_lo = np_split(0.5 * ez.reshape(128, 512))
     inv_z = np.concatenate([ez_hi, ez_hi, ez_lo], 0)
     return dict(
         fwd_z=fwd_z, by=np.stack([by_hi, by_lo], 0), tw_y=tw_y, bx=bx, tw_x=tw_x,
@@ -244,9 +244,8 @@
     return dot(jnp.concatenate([hi, lo, hi], 1), inv_z)
 
 
-def activate(value):
-    cubic = value * (0.7978845608028654 + 0.035677408136300125 * (value * value))
-    half = 0.5 * value
+def activate(half):
+    cubic = half * (1.5957691216057308 + 0.285419265090401 * (half * half))
     return half + half * jnp.tanh(cubic)
 
 
@@ -329,7 +328,7 @@
     for k in (0, 4):
         rows_ref[k:k + 3] = lift_ref[...]
         rows_ref[k + 3:k + 4] = bias_ref[...]
-    local_ref[...] = local_table(rows_ref[...], lw_ref[...], lb_ref[...])
+    local_ref[...] = 0.5 * local_table(rows_ref[...], lw_ref[...], lb_ref[...])
     lifts = lift_tables(rows_ref[...])
     for half in range(2):
         blocks = [[[w_ref[part, ky, kz, :, 512 * half:512 * half + 512] for kz in range(2)]
@@ -467,14 +466,19 @@
         for copy in fourth[piece]:
             copy.wait_recv()
         cells(start, count)
-    for copies, start_x, start_y, count in fifth:
+    for copies in [first, second] + third + meets + fourth:
+        for copy in copies:
+            copy.wait_send()
+    for part, (copies, start_x, start_y, count) in enumerate(fifth):
+        if part:
+            for copy in fifth[part - 1][0]:
+                copy.wait_send()
         for copy in copies:
             copy.wait_recv()
         cells(start_x, count)
         cells(start_y, count)
-    for copies in [first, second] + third + meets + fourth + [entry[0] for entry in fifth]:
-        for copy in copies:
-            copy.wait_send()
+    for copy in fifth[-1][0]:
+        copy.wait_send()
 
 
 def per_device(

time: 43.2 us -> 43 us (level)
  no operation moved by 1% of the time
where the time goes in v8:
time: 43 us; the launch traced here: 42.9 us
  Pallas kernels  40.9 us (95%)
  local copies, waits for them, and re-layouts  1.32 us (3%)
  between operations  0.66 us (2%)
    pallas_call x1, Pallas kernels, per_device(): pl.pallas_call(layer_kernel, out_shape=pltpu.VMEM((32, 8, 16, 256), BF16)...  40.9 us
    unnamed x1, local copies, waits for them, and re-layouts  1.32 us

profile of v8, /device:TPU:1, one launch (start us, length us, event | category | flops | bytes accessed | tf_op | source)
XLA Modules:
  0.0 42.9 jit_solution(15910285036289611445)
XLA Ops:
  0.7 40.9 %layer.1 = bf16[32,8,16,256]{3,2,1,0:T(8,128)(2,1)S(1)} custom-call(f32[1]{0:T(128)S(6)} %copy.20.refs_0_, f32[3,128,256]{2,1,0:T(8,128)} %bitcast.7, f32[3,128,256]{2,1,0:T(8,128)} %bitcast.8, bf16[64,768]{1,0:T(8,128)(2,1)} %constant.18.clone.refs_3_, bf16[2,256,512]{2,1,0:T(8,128)(2,1)} %constant.19.clone.refs_4_, f32[2,16,256]{2,1,0:T(8,128)} %constant.20.clone.refs_5_, ...), custom_call_target="tpu_custom_call" | custom-call | tf_op jit(solution)/shard_map/layer/pallas_call | solution.py:495
  41.5 1.3 %copy.19 = bf16[1,32,8,16,256]{4,3,2,1,0:T(8,128)(2,1)} copy(bf16[1,32,8,16,256]{4,3,2,1,0:T(8,128)(2,1)S(1)} %bitcast.6) | data formatting | bytes 4194304
